TPU v7x, 32 devices: a whole 2x2x4 slice. The times are simulated.
32 devices in a mesh: row: 8 (over y, x, core), col: 4 (over z).
Axes of the slice: x: 2, y: 2, z: 4, core: 2. Of those that a mesh axis runs over, the one named last changes fastest.
Arguments:
- inputs: bfloat16 [1280, 24576], P('col', 'row'), may hold values from -6 to 6
- cotangent: bfloat16 [1280, 24576], P('col', 'row'), may hold values from -6 to 6
- clip_lengths: int32 [16], P('row'), may hold values from 384 to 1536, as said below
- project_weight: float32 [3, 1280, 1280], P(None, 'row', 'col'), may hold values from -0.15625 to 0.15625
- project_moment: float32 [3, 1280, 1280], P(None, 'row', 'col'), may hold values from -80 to 80
- project_average: float32 [3, 1280, 1280], P(None, 'row', 'col'), may hold values from -0.15625 to 0.15625
- output_weight: float32 [1280, 1280], P('col', 'row'), may hold values from -1.25 to 1.25
- output_moment: float32 [1280, 1280], P('col', 'row'), may hold values from -32 to 32
- output_average: float32 [1280, 1280], P('col', 'row'), may hold values from -1.25 to 1.25
- expand_weight: float32 [1280, 5120], P('row', 'col'), may hold values from -0.15625 to 0.15625
- expand_moment: float32 [1280, 5120], P('row', 'col'), may hold values from -224 to 224
- expand_average: float32 [1280, 5120], P('row', 'col'), may hold values from -0.15625 to 0.15625
- reduce_weight: float32 [5120, 1280], P('col', 'row'), may hold values from -0.078125 to 0.078125
- reduce_moment: float32 [5120, 1280], P('col', 'row'), may hold values from -448 to 448
- reduce_average: float32 [5120, 1280], P('col', 'row'), may hold values from -0.078125 to 0.078125
- gain_first: float32 [1280], P('col'), may hold values from 0.1 to 1.9
- first_moment: float32 [1280], P('col'), may hold values from -448 to 448
- first_average: float32 [1280], P('col'), may hold values from 0.1 to 1.9
- gain_second: float32 [1280], P('col'), may hold values from 0.1 to 1.9
- second_moment: float32 [1280], P('col'), may hold values from -448 to 448
- second_average: float32 [1280], P('col'), may hold values from 0.1 to 1.9
Outputs:
- block_output: bfloat16 [1280, 24576], P('col', 'row')
- input_grad: float32 [1280, 24576], P('col', 'row')
- project_grad: float32 [3, 1280, 1280], P(None, 'row', 'col')
- project_moment_next: float32 [3, 1280, 1280], P(None, 'row', 'col')
- project_weight_next: float32 [3, 1280, 1280], P(None, 'row', 'col')
- project_average_next: float32 [3, 1280, 1280], P(None, 'row', 'col')
- project_weight_copy: bfloat16 [3, 1280, 1280], P(None, 'row', 'col')
- output_grad: float32 [1280, 1280], P('col', 'row')
- output_moment_next: float32 [1280, 1280], P('col', 'row')
- output_weight_next: float32 [1280, 1280], P('col', 'row')
- output_average_next: float32 [1280, 1280], P('col', 'row')
- output_weight_copy: bfloat16 [1280, 1280], P('col', 'row')
- expand_grad: float32 [1280, 5120], P('row', 'col')
- expand_moment_next: float32 [1280, 5120], P('row', 'col')
- expand_weight_next: float32 [1280, 5120], P('row', 'col')
- expand_average_next: float32 [1280, 5120], P('row', 'col')
- expand_weight_copy: bfloat16 [1280, 5120], P('row', 'col')
- reduce_grad: float32 [5120, 1280], P('col', 'row')
- reduce_moment_next: float32 [5120, 1280], P('col', 'row')
- reduce_weight_next: float32 [5120, 1280], P('col', 'row')
- reduce_average_next: float32 [5120, 1280], P('col', 'row')
- reduce_weight_copy: bfloat16 [5120, 1280], P('col', 'row')
- gain_first_grad: float32 [1280], P('col')
- first_moment_next: float32 [1280], P('col')
- gain_first_next: float32 [1280], P('col')
- first_average_next: float32 [1280], P('col')
- gain_second_grad: float32 [1280], P('col')
- second_moment_next: float32 [1280], P('col')
- gain_second_next: float32 [1280], P('col')
- second_average_next: float32 [1280], P('col')
Inputs may be any that keep to these rules, and one draw needn't show every extreme that they name: `clip_lengths`: real tokens of each clip; the rest of its 1536 slots is padding. Some clip is full and some holds a quarter of 1536.
All inputs are finite; a program needn't handle non-finite values.
Results may differ from a plain program's by a relative error of at most 0.02.
Values may be sent and summed in bfloat16 or wider, within the bound.
A program may use at most 256 MiB of HBM per device.

v0:
```python
import math

import jax
import jax.numpy as jnp
from jax import lax
from jax.sharding import PartitionSpec as P

HEAD_DIM = 80


EPS = 1e-05
NEG = -1e30
MOMENTUM = 0.9
AVERAGING = 0.6
RATE_PROJECT = 0.07
RATE_OUTPUT = 3.5
RATE_EXPAND = 0.06
RATE_REDUCE = 0.015
RATE_GAIN = 0.2


def contract(former, latter, former_dim, latter_dim):
    return lax.dot_general(
        former,
        latter,
        (((former_dim,), (latter_dim,)), ((), ())),
        preferred_element_type=jnp.float32,
    )


def feature_sums(former, latter):
    return lax.psum(
        (jnp.sum(former, axis=0, keepdims=True), jnp.sum(latter, axis=0, keepdims=True)), "col"
    )


def gather_features(values):
    return lax.all_gather(values, "col", axis=0, tiled=True)


def sum_features(values):
    return lax.psum_scatter(
        values.astype(jnp.bfloat16), "col", scatter_dimension=0, tiled=True
    ).astype(jnp.float32)


def normalize(values, width):
    totals, squares = feature_sums(values, values * values)
    average = totals / width
    inverse = lax.rsqrt(squares / width - average * average + EPS)
    return ((values - average) * inverse, inverse)


def normalize_back(incoming, normed, inverse, gain, width):
    scaled = incoming * gain[:, None]
    totals, crossed = feature_sums(scaled, scaled * normed)
    outgoing = inverse * (scaled - totals / width - normed * (crossed / width))
    return (outgoing, jnp.sum(incoming * normed, axis=1))


def exact_gelu(values):
    return jax.nn.gelu(values, approximate=False)


def score_block(query_block, key_rows, keys_ok):
    scores = jnp.einsum(
        "qhd,khd->hqk", query_block, key_rows, preferred_element_type=jnp.float32
    ) * (1.0 / math.sqrt(HEAD_DIM))
    return jnp.where(keys_ok[None, None, :], scores, NEG)


def attend_clip(operands):
    query_rows, key_rows, value_rows, length = operands
    seq_len = query_rows.shape[0]
    block_rows = min(512, seq_len)
    keys_ok = jnp.arange(seq_len, dtype=jnp.int32) < length

    def one_block(start):
        query_block = lax.dynamic_slice_in_dim(query_rows, start, block_rows, 0)
        scores = score_block(query_block, key_rows, keys_ok)
        highest = jnp.max(scores, axis=-1, keepdims=True)
        log_total = highest + jnp.log(jnp.sum(jnp.exp(scores - highest), axis=-1, keepdims=True))
        probs = jnp.exp(scores - log_total).astype(jnp.bfloat16)
        mixed_rows = jnp.einsum(
            "hqk,khd->qhd", probs, value_rows, preferred_element_type=jnp.float32
        )
        return (mixed_rows.astype(jnp.bfloat16), log_total[..., 0])

    starts = jnp.arange(seq_len // block_rows, dtype=jnp.int32) * block_rows
    mixed_rows, log_totals = lax.map(one_block, starts)
    return (mixed_rows.reshape(query_rows.shape), log_totals)


def attend_back(operands):
    query_rows, key_rows, value_rows, mixed_grad, log_totals, length = operands
    seq_len = query_rows.shape[0]
    block_rows = min(512, seq_len)
    keys_ok = jnp.arange(seq_len, dtype=jnp.int32) < length
    score_scale = 1.0 / math.sqrt(HEAD_DIM)

    def one_block(carry, inputs_now):
        key_grad, value_grad = carry
        start, log_total = inputs_now
        query_block = lax.dynamic_slice_in_dim(query_rows, start, block_rows, 0)
        grad_block = lax.dynamic_slice_in_dim(mixed_grad, start, block_rows, 0)
        scores = score_block(query_block, key_rows, keys_ok)
        probs = jnp.exp(scores - log_total[..., None])
        value_grad = value_grad + jnp.einsum(
            "hqk,qhd->khd",
            probs.astype(jnp.bfloat16),
            grad_block,
            preferred_element_type=jnp.float32,
        )
        prob_grad = jnp.einsum(
            "qhd,khd->hqk", grad_block, value_rows, preferred_element_type=jnp.float32
        )
        inner = jnp.sum(probs * prob_grad, axis=-1, keepdims=True)
        score_grad = (probs * (prob_grad - inner)).astype(jnp.bfloat16)
        query_grad = (
            jnp.einsum("hqk,khd->qhd", score_grad, key_rows, preferred_element_type=jnp.float32)
            * score_scale
        )
        key_grad = (
            key_grad
            + jnp.einsum(
                "hqk,qhd->khd", score_grad, query_block, preferred_element_type=jnp.float32
            )
            * score_scale
        )
        return ((key_grad, value_grad), query_grad.astype(jnp.bfloat16))

    starts = jnp.arange(seq_len // block_rows, dtype=jnp.int32) * block_rows
    zeros_init = jnp.zeros(key_rows.shape, jnp.float32)
    (key_grad, value_grad), query_grad = lax.scan(
        one_block, (zeros_init, zeros_init), (starts, log_totals)
    )
    return (
        query_grad.reshape(query_rows.shape),
        key_grad.astype(jnp.bfloat16),
        value_grad.astype(jnp.bfloat16),
    )


def update(weight, moment, average, gradient, rate):
    moment_next = MOMENTUM * moment + gradient
    weight_next = weight - rate * (gradient + MOMENTUM * moment_next)
    average_next = AVERAGING * average + (1.0 - AVERAGING) * weight_next
    return (moment_next, weight_next, average_next)


def on_device(
    inputs,
    cotangent,
    clip_lengths,
    project_weight,
    project_moment,
    project_average,
    output_weight,
    output_moment,
    output_average,
    expand_weight,
    expand_moment,
    expand_average,
    reduce_weight,
    reduce_moment,
    reduce_average,
    gain_first,
    first_moment,
    first_average,
    gain_second,
    second_moment,
    second_average,
):
    block_width, rows_local = inputs.shape
    width = block_width * lax.axis_size("col")
    clips_local = clip_lengths.shape[0]
    seq_len = rows_local // clips_local
    head_count = block_width // HEAD_DIM
    positions = jnp.arange(seq_len, dtype=jnp.int32)
    row_mask = (
        (positions[None, :] < clip_lengths[:, None]).astype(jnp.float32).reshape(1, rows_local)
    )
    resident = inputs.astype(jnp.float32)
    normed_one, inverse_one = normalize(resident, width)
    full_one = gather_features((normed_one * gain_first[:, None]).astype(jnp.bfloat16))
    project_full, output_full, expand_full, reduce_full = (
        lax.all_gather(project_weight.astype(jnp.bfloat16), "row", axis=1, tiled=True),
        lax.all_gather(output_weight.astype(jnp.bfloat16), "row", axis=1, tiled=True),
        lax.all_gather(expand_weight.astype(jnp.bfloat16), "row", axis=0, tiled=True),
        lax.all_gather(reduce_weight.astype(jnp.bfloat16), "row", axis=1, tiled=True),
    )
    projected = jnp.einsum(
        "dt,kde->kte", full_one, project_full, preferred_element_type=jnp.float32
    ).astype(jnp.bfloat16)
    split_rows = projected.reshape(3, clips_local, seq_len, head_count, HEAD_DIM)
    attended, log_totals = lax.map(
        attend_clip, (split_rows[0], split_rows[1], split_rows[2], clip_lengths)
    )
    attended_rows = attended.reshape(rows_local, block_width)
    middle = resident + sum_features(contract(output_full, attended_rows, 0, 1))
    normed_two, inverse_two = normalize(middle, width)
    full_two = gather_features((normed_two * gain_second[:, None]).astype(jnp.bfloat16))
    pre_act = contract(full_two, expand_full, 0, 0)
    activated, gelu_back = jax.vjp(exact_gelu, pre_act)
    activated = activated.astype(jnp.bfloat16)
    block_output = (middle + sum_features(contract(reduce_full, activated, 0, 1))).astype(
        jnp.bfloat16
    )
    project_back, output_back, expand_back, reduce_back = (
        project_full,
        output_full,
        expand_full,
        reduce_full,
    )
    upstream = cotangent.astype(jnp.float32) * row_mask
    upstream_full = gather_features(upstream.astype(jnp.bfloat16))
    hidden_grad = contract(upstream_full, reduce_back, 0, 1)
    reduce_part = contract(activated, upstream_full, 0, 1)
    pre_grad = gelu_back(hidden_grad)[0].astype(jnp.bfloat16)
    expand_part = contract(full_two, pre_grad, 1, 0)
    normed_two_grad = sum_features(contract(expand_back, pre_grad, 1, 1))
    middle_grad, gain_two_part = normalize_back(
        normed_two_grad, normed_two, inverse_two, gain_second, width
    )
    middle_grad = middle_grad + upstream
    middle_full_grad = gather_features(middle_grad.astype(jnp.bfloat16))
    output_part = contract(attended_rows, middle_full_grad, 0, 1)
    attended_grad = contract(middle_full_grad, output_back, 0, 1).astype(jnp.bfloat16)
    grad_split = attended_grad.reshape(clips_local, seq_len, head_count, HEAD_DIM)
    query_grad, key_grad, value_grad = lax.map(
        attend_back,
        (split_rows[0], split_rows[1], split_rows[2], grad_split, log_totals, clip_lengths),
    )
    stacked_grad = jnp.stack([query_grad, key_grad, value_grad]).reshape(3, rows_local, block_width)
    normed_one_grad = sum_features(
        jnp.einsum("kte,kde->dt", stacked_grad, project_back, preferred_element_type=jnp.float32)
    )
    project_part = jnp.einsum(
        "dt,kte->kde", full_one, stacked_grad, preferred_element_type=jnp.float32
    )
    input_grad, gain_one_part = normalize_back(
        normed_one_grad, normed_one, inverse_one, gain_first, width
    )
    input_grad = input_grad + middle_grad
    project_grad, output_grad, expand_grad, reduce_grad = (
        lax.psum_scatter(
            project_part.astype(jnp.bfloat16), "row", scatter_dimension=1, tiled=True
        ).astype(jnp.float32),
        lax.psum_scatter(
            output_part.astype(jnp.bfloat16), "row", scatter_dimension=1, tiled=True
        ).astype(jnp.float32),
        lax.psum_scatter(
            expand_part.astype(jnp.bfloat16), "row", scatter_dimension=0, tiled=True
        ).astype(jnp.float32),
        lax.psum_scatter(
            reduce_part.astype(jnp.bfloat16), "row", scatter_dimension=1, tiled=True
        ).astype(jnp.float32),
    )
    gain_one_grad, gain_two_grad = lax.psum((gain_one_part, gain_two_part), "row")
    scale = 1.0 / math.sqrt(rows_local * lax.axis_size("row"))
    pm, pw, pa = update(
        project_weight, project_moment, project_average, project_grad, RATE_PROJECT * scale
    )
    om, ow, oa = update(
        output_weight, output_moment, output_average, output_grad, RATE_OUTPUT * scale
    )
    em, ew, ea = update(
        expand_weight, expand_moment, expand_average, expand_grad, RATE_EXPAND * scale
    )
    rm, rw, ra = update(
        reduce_weight, reduce_moment, reduce_average, reduce_grad, RATE_REDUCE * scale
    )
    fm, fw, fa = update(gain_first, first_moment, first_average, gain_one_grad, RATE_GAIN * scale)
    sm, sw, sa = update(
        gain_second, second_moment, second_average, gain_two_grad, RATE_GAIN * scale
    )
    return (
        block_output,
        input_grad,
        project_grad,
        pm,
        pw,
        pa,
        pw.astype(jnp.bfloat16),
        output_grad,
        om,
        ow,
        oa,
        ow.astype(jnp.bfloat16),
        expand_grad,
        em,
        ew,
        ea,
        ew.astype(jnp.bfloat16),
        reduce_grad,
        rm,
        rw,
        ra,
        rw.astype(jnp.bfloat16),
        gain_one_grad,
        fm,
        fw,
        fa,
        gain_two_grad,
        sm,
        sw,
        sa,
    )


def solution(mesh):
    placed = (
        P("col", "row"),
        P("col", "row"),
        P("row"),
        P(None, "row", "col"),
        P(None, "row", "col"),
        P(None, "row", "col"),
        P("col", "row"),
        P("col", "row"),
        P("col", "row"),
        P("row", "col"),
        P("row", "col"),
        P("row", "col"),
        P("col", "row"),
        P("col", "row"),
        P("col", "row"),
        P("col"),
        P("col"),
        P("col"),
        P("col"),
        P("col"),
        P("col"),
    )
    return jax.shard_map(
        on_device,
        mesh=mesh,
        in_specs=placed,
        out_specs=(
            P("col", "row"),
            P("col", "row"),
            P(None, "row", "col"),
            P(None, "row", "col"),
            P(None, "row", "col"),
            P(None, "row", "col"),
            P(None, "row", "col"),
            P("col", "row"),
            P("col", "row"),
            P("col", "row"),
            P("col", "row"),
            P("col", "row"),
            P("row", "col"),
            P("row", "col"),
            P("row", "col"),
            P("row", "col"),
            P("row", "col"),
            P("col", "row"),
            P("col", "row"),
            P("col", "row"),
            P("col", "row"),
            P("col", "row"),
            P("col"),
            P("col"),
            P("col"),
            P("col"),
            P("col"),
            P("col"),
            P("col"),
            P("col"),
        ),
        check_vma=False,
    )
```

profile of v0, /device:TPU:8, one launch (start us, length us, event | category | flops | bytes accessed | tf_op | source)
XLA Modules:
  0.0 1813.4 jit_solution(11088466728528908229)
XLA Ops:
  11.5 15.6 all-reduce.4
  30.5 16.3 all_gather.26
  46.7 140.5 %all-gather.8.cloned.1.call-done = bf16[1280,3072]{1,0:T(8,128)(2,1)} async-done(((bf16[320,3072]{1,0:T(8,128)(2,1)}), bf16[1280,3072]{1,0:T(8,128)(2,1)}) %all-gather.8.cloned.1.call-update) | async-done | bytes 7864336 | tf_op jit(solution)/shard_map/all_gather | solution.py:38
  187.3 11.2 convert_bitcast_fusion
  226.4 97.3 %while.55 = (s32[]{:T(128)}, bf16[2,1536,4,80]{3,2,1,0:T(4,128)(2,1)}, f32[2,3,4,512]{3,2,1,0:T(4,128)}, bf16[2,1536,4,80]{1,3,2,0:T(8,128)(2,1)}, bf16[2,1536,4...) while((s32[]{:T(128)}, ...), condition=%wide.region_9.10_spmd, body=%wide.region_4.9_spmd.sunk | while | flops 1041399296 | bytes 50912180 | solution.py:196
  231.9 38.6 %while.58 = (s32[]{:T(128)}, bf16[3,512,4,80]{1,3,2,0:T(8,128)(2,1)}, f32[3,4,512]{2,1,0:T(4,128)S(1)}, s32[3]{0:T(128)S(1)}, bf16[1536,4,80]{0,2,1:T(8,128)(2,1...) while((s32[]{:T(128)}, ...), condition=%wide.region_8.8_spmd.clone, body=%wide.region_5.7_spmd.clone.sunk | while | flops 1041399296 | bytes 40442544 | solution.py:90
  280.4 38.6 %while.58 = (s32[]{:T(128)}, bf16[3,512,4,80]{1,3,2,0:T(8,128)(2,1)}, f32[3,4,512]{2,1,0:T(4,128)S(1)}, s32[3]{0:T(128)S(1)}, bf16[1536,4,80]{0,2,1:T(8,128)(2,1...) while((s32[]{:T(128)}, ...), condition=%wide.region_8.8_spmd.clone, body=%wide.region_5.7_spmd.clone.sunk | while | flops 1041399296 | bytes 40442544 | solution.py:90
  337.3 135.6 %reduce-scatter.11.cloned.1.call-done = bf16[320,3072]{1,0:T(8,128)(2,1)} async-done(((bf16[1280,3072]{1,0:T(8,128)(2,1)}), bf16[320,3072]{1,0:T(8,128)(2,1)}) %reduce-scatter.11.cloned.1.call-update) | async-done | bytes 1966096 | tf_op jit(solution)/shard_map/reduce_scatter | solution.py:42
  475.3 15.2 all-reduce.3
  498.5 10.0 all-gather.14.cloned.1.call-done
  508.5 140.1 %all-gather.12.cloned.1.call-done = bf16[1280,3072]{1,0:T(8,128)(2,1)} async-done(((bf16[320,3072]{1,0:T(8,128)(2,1)}), bf16[1280,3072]{1,0:T(8,128)(2,1)}) %all-gather.12.cloned.1.call-update) | async-done | bytes 7864336 | tf_op jit(solution)/shard_map/all_gather | solution.py:38
  648.6 16.9 fusion.91
  665.5 19.4 %all-gather.16.cloned.1.call-done = bf16[1280,1280]{0,1:T(8,128)(2,1)} async-done(((bf16[1280,160]{0,1:T(8,128)(2,1)}), bf16[1280,1280]{0,1:T(8,128)(2,1)}) %all-gather.16.cloned.1.call-update) | async-done | bytes 3276816 | tf_op jit(solution)/shard_map/all_gather | solution.py:190
  684.8 140.3 %all-gather.18.cloned.1.call-done = bf16[1280,3072]{1,0:T(8,128)(2,1)} async-done(((bf16[320,3072]{1,0:T(8,128)(2,1)}), bf16[1280,3072]{1,0:T(8,128)(2,1)}) %all-gather.18.cloned.1.call-update) | async-done | bytes 7864336 | tf_op jit(solution)/shard_map/all_gather | solution.py:38
  825.1 52.0 %add_convert_fusion = (bf16[3072,1280]{1,0:T(8,128)(2,1)S(1)}, f32[3072,1280]{1,0:T(8,128)}) fusion(f32[3072,1280]{1,0:T(8,128)} %fusion.91, bf16[1280,3072]{1,0:T(8,128)(2,1)} %all-gather.18.cloned.1.call-done, bf16[1280,1280]{0,1:T(8,128)(2,1)} %all-gather.16.cloned.1.call-done), kind=kOutput, calls=%fused_computation.62 | convolution fusion | flops 10349445120 | bytes 50462720 | tf_op jit(solution)/shard_map/dot_general | solution.py:23
  880.2 12.4 fusion.44
  892.9 137.3 %reduce-scatter.15.cloned.1.call-done = bf16[320,3072]{1,0:T(8,128)(2,1)} async-done(((bf16[1280,3072]{1,0:T(8,128)(2,1)}), bf16[320,3072]{1,0:T(8,128)(2,1)}) %reduce-scatter.15.cloned.1.call-update) | async-done | bytes 1966096 | tf_op jit(solution)/shard_map/reduce_scatter | solution.py:42
  1035.4 14.8 all-reduce.2
  1056.9 16.1 convolution_convert_fusion.4
  1073.6 10.9 multiply_convert_fusion.1
  1087.6 14.1 convolution_convert_fusion.3
  1101.7 95.1 %all-gather.20.cloned.1.call-done = bf16[1280,3072]{1,0:T(8,128)(2,1)} async-done(((bf16[320,3072]{1,0:T(8,128)(2,1)}), bf16[1280,3072]{1,0:T(8,128)(2,1)}) %all-gather.20.cloned.1.call-update) | async-done | bytes 7864336 | tf_op jit(solution)/shard_map/all_gather | solution.py:38
  1213.2 191.9 %while.57 = (s32[]{:T(128)}, bf16[2,1536,4,80]{3,2,1,0:T(4,128)(2,1)}, bf16[2,1536,4,80]{1,3,2,0:T(8,128)(2,1)}, bf16[2,1536,4,80]{1,3,2,0:T(8,128)(2,1)}, f32[2...) while((s32[]{:T(128)}, ...), condition=%wide.region_25.26_spmd, body=%wide.region_21.25_spmd.sunk | while | flops 2548661760 | bytes 154889840 | solution.py:230
  1223.1 77.2 %while.59 = (s32[]{:T(128)}, f32[1536,4,80]{0,2,1:T(8,128)}, f32[1536,4,80]{0,2,1:T(8,128)S(1)}, bf16[3,512,4,80]{1,3,2,0:T(8,128)(2,1)}, s32[3]{0:T(128)S(1)}, ...) while((s32[]{:T(128)}, f32[1536,4,80]{0,2,1:T(8,128)}, ...), condition=%wide.region_24.24_spmd.clone, body=%wide.region_22.23_spmd.clone.sunk | while | flops 2547678720 | bytes 135965984 | solution.py:134
  1319.3 76.5 %while.59 = (s32[]{:T(128)}, f32[1536,4,80]{0,2,1:T(8,128)}, f32[1536,4,80]{0,2,1:T(8,128)S(1)}, bf16[3,512,4,80]{1,3,2,0:T(8,128)(2,1)}, s32[3]{0:T(128)S(1)}, ...) while((s32[]{:T(128)}, f32[1536,4,80]{0,2,1:T(8,128)}, ...), condition=%wide.region_24.24_spmd.clone, body=%wide.region_22.23_spmd.clone.sunk | while | flops 2547678720 | bytes 135965984 | solution.py:134
  1436.9 13.2 fusion.79
  1464.7 12.9 fusion.46
  1479.5 15.7 fusion.43
  1535.9 123.1 %reduce-scatter.17.cloned.1.call-done = bf16[320,3072]{1,0:T(8,128)(2,1)} async-done(((bf16[1280,3072]{1,0:T(8,128)(2,1)}), bf16[320,3072]{1,0:T(8,128)(2,1)}) %reduce-scatter.17.cloned.1.call-update) | async-done | bytes 1966096 | tf_op jit(solution)/shard_map/reduce_scatter | solution.py:42
  1662.7 13.6 all-reduce
  1676.3 25.1 %all-reduce.1 = (f32[1,3072]{1,0:T(1,128)S(1)}, f32[1,3072]{1,0:T(1,128)S(1)}) all-reduce(f32[1,3072]{1,0:T(1,128)S(1)} %bitcast.221, f32[1,3072]{1,0:T(1,128)S(1)} %bitcast.222), channel_id=1, replica_groups=mesh['row'=8,'col'=4] {'col'}, use_global_device_ids=true, to_apply=%region_30.31 | all-reduce | flops 6144 | bytes 49152 | tf_op jit(solution)/shard_map/psum | solution.py:32
  1702.6 96.4 %reduce-scatter.13.cloned.1.call-done = bf16[320,3072]{1,0:T(8,128)(2,1)} async-done(((bf16[1280,3072]{1,0:T(8,128)(2,1)}), bf16[320,3072]{1,0:T(8,128)(2,1)}) %reduce-scatter.13.cloned.1.call-update) | async-done | bytes 1966096 | tf_op jit(solution)/shard_map/reduce_scatter | solution.py:42
  (367 shorter events, 460.7 us)
Async XLA Ops:
  7.2 39.5 %all-gather.10.cloned.1.call-start = ((), (), s32[]{:S(2)}) async-start(), calls=%async_computation.9 | async-start | bytes 3317760 | tf_op jit(solution)/shard_map/all_gather | solution.py:187
  9.3 177.9 %all-gather.8.cloned.1.call-start = ((), (), s32[]{:S(2)}) async-start(), calls=%async_computation.8 | async-start | bytes 9830400 | tf_op jit(solution)/shard_map/all_gather | solution.py:38
  30.4 442.5 %reduce-scatter.11.cloned.1.call-start = ((), (), s32[]{:S(2)}) async-start(), calls=%async_computation.10 | async-start | bytes 9830400 | tf_op jit(solution)/shard_map/reduce_scatter | solution.py:42
  335.4 155.8 %copy-start.42 = (f32[320]{0:T(512)S(1)}, f32[320]{0:T(512)}, u32[]{:S(2)}) copy-start(f32[320]{0:T(512)} %param.47) | copy-start | bytes 3844
  335.4 173.2 %all-gather.14.cloned.1.call-start = ((), (), s32[]{:S(2)}) async-start(), calls=%async_computation.12 | async-start | bytes 3686400 | tf_op jit(solution)/shard_map/all_gather | solution.py:189
  337.3 311.3 %all-gather.12.cloned.1.call-start = ((), (), s32[]{:S(2)}) async-start(), calls=%async_computation.11 | async-start | bytes 9830400 | tf_op jit(solution)/shard_map/all_gather | solution.py:38
  495.0 189.9 %all-gather.16.cloned.1.call-start = ((), (), s32[]{:S(2)}) async-start(), calls=%async_computation.13 | async-start | bytes 3686400 | tf_op jit(solution)/shard_map/all_gather | solution.py:190
  495.9 329.2 %all-gather.18.cloned.1.call-start = ((), (), s32[]{:S(2)}) async-start(), calls=%async_computation.15 | async-start | bytes 9830400 | tf_op jit(solution)/shard_map/all_gather | solution.py:38
  496.7 168.8 %copy-start.31 = (f32[3072]{0:T(1024)}, f32[3072]{0:T(1024)S(1)}, u32[]{:S(2)}) copy-start(f32[3072]{0:T(1024)S(1)} %reshape.138) | copy-start | bytes 36868
  498.5 531.7 %reduce-scatter.15.cloned.1.call-start = ((), (), s32[]{:S(2)}) async-start(), calls=%async_computation.16 | async-start | bytes 9830400 | tf_op jit(solution)/shard_map/reduce_scatter | solution.py:42
  684.8 195.3 %copy-start.54 = (bf16[1280,1280]{1,0:T(8,128)(2,1)S(1)}, bf16[1280,1280]{1,0:T(8,128)(2,1)}, u32[]{:S(2)}) copy-start(bf16[1280,1280]{1,0:T(8,128)(2,1)} %all-gather.14.cloned.1.call-done) | copy-start | bytes 9830404
  892.6 137.6 %copy-start.25 = (f32[1,3072]{1,0:T(1,128)S(1)}, f32[1,3072]{1,0:T(1,128)}, u32[]{:S(2)}) copy-start(f32[1,3072]{1,0:T(1,128)} %copy-done.24) | copy-start | bytes 36868
  892.6 137.6 %copy-start.28 = (f32[1,3072]{1,0:T(1,128)S(1)}, f32[1,3072]{1,0:T(1,128)}, u32[]{:S(2)}) copy-start(f32[1,3072]{1,0:T(1,128)} %copy-done.27) | copy-start | bytes 36868
  892.6 137.6 %copy-start.43 = (f32[320]{0:T(512)S(1)}, f32[320]{0:T(512)}, u32[]{:S(2)}) copy-start(f32[320]{0:T(512)} %param.47) | copy-start | bytes 3844
  892.6 158.2 %copy-start.32 = (f32[3072]{0:T(1024)S(1)}, f32[3072]{0:T(1024)}, u32[]{:S(2)}) copy-start(f32[3072]{0:T(1024)} %copy-done.31) | copy-start | bytes 36868
  892.6 304.2 %all-gather.20.cloned.1.call-start = ((), (), s32[]{:S(2)}) async-start(), calls=%async_computation.17 | async-start | bytes 9830400 | tf_op jit(solution)/shard_map/all_gather | solution.py:38
  1056.9 444.7 %reduce-scatter.21.cloned.1.call-start = ((), (), s32[]{:S(2)}) async-start(), calls=%async_computation.20 | async-start | bytes 3686400 | tf_op jit(solution)/shard_map/reduce_scatter | solution.py:252
  1073.0 434.4 %reduce-scatter.23.cloned.1.call-start = ((), (), s32[]{:S(2)}) async-start(), calls=%async_computation.21 | async-start | bytes 3686400 | tf_op jit(solution)/shard_map/reduce_scatter | solution.py:255
  1101.7 411.0 %reduce-scatter.19.cloned.1.call-start = ((), (), s32[]{:S(2)}) async-start(), calls=%async_computation.19 | async-start | bytes 1105920 | tf_op jit(solution)/shard_map/reduce_scatter | solution.py:249
  1436.9 83.7 %reduce-scatter.25.cloned.1.call-start = ((), (), s32[]{:S(2)}) async-start(), calls=%async_computation.22 | async-start | bytes 2949120
  1464.6 194.5 %reduce-scatter.17.cloned.1.call-start = ((), (), s32[]{:S(2)}) async-start(), calls=%async_computation.18 | async-start | bytes 9830400 | tf_op jit(solution)/shard_map/reduce_scatter | solution.py:42
  1477.6 321.4 %reduce-scatter.13.cloned.1.call-start = ((), (), s32[]{:S(2)}) async-start(), calls=%async_computation.14 | async-start | bytes 9830400 | tf_op jit(solution)/shard_map/reduce_scatter | solution.py:42
  1529.6 171.8 %copy-start.47 = (f32[320]{0:T(512)S(1)}, f32[320]{0:T(512)}, u32[]{:S(2)}) copy-start(f32[320]{0:T(512)} %param.46) | copy-start | bytes 3844
  1529.6 171.8 %copy-start.48 = (f32[320]{0:T(512)S(1)}, f32[320]{0:T(512)}, u32[]{:S(2)}) copy-start(f32[320]{0:T(512)} %param.45) | copy-start | bytes 3844
  1529.6 172.4 %copy-start.44 = (f32[320]{0:T(512)S(1)}, f32[320]{0:T(512)}, u32[]{:S(2)}) copy-start(f32[320]{0:T(512)} %param.47) | copy-start | bytes 3844
  1529.6 172.4 %copy-start.49 = (f32[320]{0:T(512)S(1)}, f32[320]{0:T(512)}, u32[]{:S(2)}) copy-start(f32[320]{0:T(512)} %param.49) | copy-start | bytes 3844
  1529.6 172.4 %copy-start.50 = (f32[320]{0:T(512)S(1)}, f32[320]{0:T(512)}, u32[]{:S(2)}) copy-start(f32[320]{0:T(512)} %param.48) | copy-start | bytes 3844
  1529.6 269.4 %copy-start.26 = (f32[1,3072]{1,0:T(1,128)S(1)}, f32[1,3072]{1,0:T(1,128)}, u32[]{:S(2)}) copy-start(f32[1,3072]{1,0:T(1,128)} %copy-done.24) | copy-start | bytes 36868
  1529.7 269.4 %copy-start.29 = (f32[1,3072]{1,0:T(1,128)S(1)}, f32[1,3072]{1,0:T(1,128)}, u32[]{:S(2)}) copy-start(f32[1,3072]{1,0:T(1,128)} %copy-done.27) | copy-start | bytes 36868
  1529.7 269.4 %copy-start.33 = (f32[3072]{0:T(1024)S(1)}, f32[3072]{0:T(1024)}, u32[]{:S(2)}) copy-start(f32[3072]{0:T(1024)} %copy-done.31) | copy-start | bytes 36868
  1529.7 269.4 %copy-start.39 = (f32[1,3072]{1,0:T(1,128)S(1)}, f32[1,3072]{1,0:T(1,128)}, u32[]{:S(2)}) copy-start(f32[1,3072]{1,0:T(1,128)} %copy-done.38) | copy-start | bytes 36868
  1529.7 269.4 %copy-start.41 = (f32[1,3072]{1,0:T(1,128)S(1)}, f32[1,3072]{1,0:T(1,128)}, u32[]{:S(2)}) copy-start(f32[1,3072]{1,0:T(1,128)} %copy-done.40) | copy-start | bytes 36868
  (49 other events, 1482.1 us)
Sparse Core Ops, SparseCore 0:
  10.5 36.2 all-gather.9
  48.9 138.3 all-gather.7
  335.5 137.4 reduce-scatter.10
  475.2 33.2 all-gather.13
  510.5 138.0 all-gather.11
  650.9 33.8 all-gather.15
  687.0 138.0 all-gather.17
  892.7 137.4 reduce-scatter.14
  1057.0 139.8 all-gather.19
  1200.1 47.8 reduce-scatter.20
  1251.4 46.7 reduce-scatter.22
  1437.0 36.7 reduce-scatter.18
  1477.1 43.4 reduce-scatter.24
  1522.8 136.2 reduce-scatter.16
  1661.2 137.8 reduce-scatter.12
where the time goes:
time: 1830 us; the launch traced here: 1810 us
  waiting for transfers between devices  1040 us (57%)
  matrix products  338 us (18%)
  local copies, waits for them, and re-layouts  171 us (9%)
  other arithmetic  122 us (7%)
  blocking collectives  101 us (6%)
  loops' own time  24.3 us (1%)
    all_gather x4, waiting for transfers between devices, gather_features(): return lax.all_gather(values, 'col', axis=0, tiled=True)  516 us
    reduce_scatter x4, waiting for transfers between devices, sum_features(): lax.psum_scatter(values.astype(jnp.bfloat16), 'col', scatter_dimension=0,...  492 us
    dot_general x9, matrix products, contract(): lax.dot_general(former, latter, (((former_dim,), (latter_dim,)), ((), ())...  149 us
    psum x4, blocking collectives, feature_sums(): lax.psum((jnp.sum(former, axis=0, keepdims=True), jnp.sum(latter, axis=0,...  70.7 us
    dot_general x12, matrix products, score_block(): jnp.einsum('qhd,khd->hqk', query_block, key_rows, preferred_element_type=...  48 us
    unnamed x120, local copies, waits for them, and re-layouts  43 us
  transfers between devices with their start and end apart: 15, of which 11 were waited for; matrix products, arithmetic and copies ran while one was open for 22% of the time, Pallas kernels for 0%

commit v1 on v0

v1 whole, which is shorter than its diff:
```python
import functools
import math

import jax
import jax.numpy as jnp
from jax import lax
from jax.experimental import pallas as pl
from jax.experimental.pallas import tpu as pltpu
from jax.sharding import Mesh
from jax.sharding import PartitionSpec as P

HEAD_DIM = 80


EPS = 1e-05
NEG = -1e30
MOMENTUM = 0.9
AVERAGING = 0.6
RATE_PROJECT = 0.07
RATE_OUTPUT = 3.5
RATE_EXPAND = 0.06
RATE_REDUCE = 0.015
RATE_GAIN = 0.2

CLIPS_PER_COLUMN = 4
ROW = ("pair", "core")
COL = ("zhi", "zlo")
COLUMN = ("core", "zhi", "zlo")
TEAM = ("core", "zlo")
EVERY = ("zhi", "zlo", "pair", "core")
SPARE = 16


def exchange(values, axes, step, size):
    return lax.ppermute(values, axes, [(at, at ^ step) for at in range(size)])


def column_pairs(depth, step):
    team = depth // 2
    half = team // 2
    pairs = []
    for core in range(2):
        for place in range(depth):
            chunk = place ^ step
            clip, slot = divmod(chunk, team)
            to_core, low = divmod(slot, half)
            to_place = (2 * core + clip) * (depth // CLIPS_PER_COLUMN) + low
            pairs.append((core * depth + place, to_core * depth + to_place))
    return pairs


def own_chunk(depth):
    team = depth // 2
    place = lax.axis_index(COL)
    per_clip = depth // CLIPS_PER_COLUMN
    clip = (place // per_clip) % 2
    slot = lax.axis_index("core") * (team // 2) + place % per_clip
    return clip * team + slot


def to_tokens(values, depth):
    width, rows = values.shape
    size = rows // depth
    place = lax.axis_index(COL)
    mine = own_chunk(depth)
    pieces = []
    for step in range(depth):
        chunk = lax.dynamic_slice_in_dim(values, (place ^ step) * size, size, 1)
        pieces.append(lax.ppermute(chunk, COLUMN, column_pairs(depth, step)))
    stacked = jnp.stack(pieces)
    order = [lax.dynamic_index_in_dim(stacked, at ^ mine, 0, False) for at in range(depth)]
    return jnp.concatenate(order, axis=0)


def to_features(values, depth):
    width, size = values.shape
    block = width // depth
    place = lax.axis_index(COL)
    mine = own_chunk(depth)
    whole = jnp.zeros((block, size * depth), values.dtype)
    for step in range(depth):
        chunk = lax.dynamic_slice_in_dim(values, (mine ^ step) * block, block, 0)
        back = [(target, source) for source, target in column_pairs(depth, step)]
        piece = lax.ppermute(chunk, COLUMN, back)
        whole = lax.dynamic_update_slice_in_dim(whole, piece, (place ^ step) * size, 1)
    return whole


def attend_kernel(team, valid_ref, *refs):
    query_ref, keys, values = refs[0], refs[1 : 1 + team], refs[1 + team : 1 + 2 * team]
    out_ref, log_ref, wide_keys, wide_values = refs[1 + 2 * team :]
    dim, size = query_ref.shape
    scale = math.log2(math.e) / math.sqrt(HEAD_DIM)
    pad = (SPARE, size)
    row = lax.broadcasted_iota(jnp.int32, pad, 0)
    position = lax.broadcasted_iota(jnp.int32, pad, 1)
    for at in range(team):
        own = keys[at][...]
        bias = jnp.where((row == 0) & (position >= valid_ref[at]), NEG, 0.0).astype(jnp.bfloat16)
        wide = jnp.concatenate([own, own, bias], axis=0)
        wide_keys[pl.ds(at * size, size), :] = wide.T
        ones = jnp.where(row == 0, 1.0, 0.0).astype(jnp.bfloat16)
        wide_values[:, pl.ds(at * size, size)] = jnp.concatenate([values[at][...], ones], axis=0)
    block = 256 if size % 256 == 0 else 128
    for start in range(0, size, block):
        query = query_ref[:, pl.ds(start, block)].astype(jnp.float32) * scale
        high = query.astype(jnp.bfloat16)
        low = (query - high.astype(jnp.float32)).astype(jnp.bfloat16)
        one = jnp.where(
            lax.broadcasted_iota(jnp.int32, (SPARE, block), 0) == 0, 1.0, 0.0
        ).astype(jnp.bfloat16)
        wide_query = jnp.concatenate([high, low, one], axis=0)
        scores = jnp.dot(wide_keys[...], wide_query, preferred_element_type=jnp.float32)
        highest = jnp.max(scores, axis=0, keepdims=True)
        powers = jnp.exp2(scores - highest).astype(jnp.bfloat16)
        mixed = jnp.dot(wide_values[...], powers, preferred_element_type=jnp.float32)
        total = mixed[dim : dim + 1]
        out_ref[:, pl.ds(start, block)] = (mixed[:dim] / total).astype(jnp.bfloat16)
        log_ref[0, :, pl.ds(start, block)] = highest + jnp.log2(total)


def three_parts(values):
    high = values.astype(jnp.bfloat16)
    rest = values - high.astype(jnp.float32)
    middle = rest.astype(jnp.bfloat16)
    low = (rest - middle.astype(jnp.float32)).astype(jnp.bfloat16)
    return high, middle, low


def spare_rows(first, parts, block):
    row = lax.broadcasted_iota(jnp.int32, (SPARE, block), 0)
    rows = jnp.where(row == 0, first, 0.0)
    for at, part in enumerate(parts):
        rows = jnp.where(row == at + 1, -part.astype(jnp.float32), rows)
    return rows.astype(jnp.bfloat16)


def attend_back_kernel(team, valid_ref, *refs):
    query_ref, out_ref, grad_ref, log_ref = refs[:4]
    keys, values = refs[4 : 4 + team], refs[4 + team : 4 + 2 * team]
    query_grad_ref = refs[4 + 2 * team]
    key_grads = refs[5 + 2 * team : 5 + 3 * team]
    value_grads = refs[5 + 3 * team : 5 + 4 * team]
    wide_keys, wide_values, flat_keys, key_total, value_total = refs[5 + 4 * team :]
    dim, size = query_ref.shape
    base = 1.0 / math.sqrt(HEAD_DIM)
    scale = math.log2(math.e) * base
    pad = (SPARE, size)
    row = lax.broadcasted_iota(jnp.int32, pad, 0)
    position = lax.broadcasted_iota(jnp.int32, pad, 1)
    for at in range(team):
        own = keys[at][...]
        outside = position >= valid_ref[at]
        bias = jnp.where(
            row == 0, jnp.where(outside, NEG, 0.0), jnp.where(row < 4, 1.0, 0.0)
        ).astype(jnp.bfloat16)
        wide_keys[pl.ds(at * size, size), :] = jnp.concatenate([own, own, bias], axis=0).T
        flat_keys[:, pl.ds(at * size, size)] = own
        ones = jnp.where((row >= 1) & (row < 4), 1.0, 0.0).astype(jnp.bfloat16)
        wide_values[pl.ds(at * size, size), :] = jnp.concatenate(
            [values[at][...], ones], axis=0
        ).T
    block = 256 if size % 256 == 0 else 128
    for start in range(0, size, block):
        here = pl.ds(start, block)
        raw = query_ref[:, here]
        query = raw.astype(jnp.float32) * scale
        high = query.astype(jnp.bfloat16)
        low = (query - high.astype(jnp.float32)).astype(jnp.bfloat16)
        grad = grad_ref[:, here]
        inner = jnp.sum(
            grad.astype(jnp.float32) * out_ref[:, here].astype(jnp.float32), axis=0, keepdims=True
        )
        wide_query = jnp.concatenate(
            [high, low, spare_rows(1.0, three_parts(log_ref[0, :, here]), block)], axis=0
        )
        wide_grad = jnp.concatenate([grad, spare_rows(0.0, three_parts(inner), block)], axis=0)
        scores = jnp.dot(wide_keys[...], wide_query, preferred_element_type=jnp.float32)
        probs = jnp.exp2(scores)
        prob_grad = jnp.dot(wide_values[...], wide_grad, preferred_element_type=jnp.float32)
        score_grad = (probs * prob_grad).astype(jnp.bfloat16)
        probs = probs.astype(jnp.bfloat16)
        query_grad_ref[:, here] = (
            jnp.dot(flat_keys[...], score_grad, preferred_element_type=jnp.float32) * base
        ).astype(jnp.bfloat16)
        value_part = jnp.dot(probs, grad.T, preferred_element_type=jnp.float32)
        key_part = jnp.dot(score_grad, raw.T, preferred_element_type=jnp.float32)
        if start == 0:
            value_total[...] = value_part
            key_total[...] = key_part
        else:
            value_total[...] += value_part
            key_total[...] += key_part
    for at in range(team):
        part = pl.ds(at * size, size)
        key_grads[at][...] = (key_total[part, :] * base).T.astype(jnp.bfloat16)
        value_grads[at][...] = value_total[part, :].T.astype(jnp.bfloat16)


def head_specs(size, count):
    return [pl.BlockSpec((HEAD_DIM, size), lambda head, *_: (head, 0)) for _ in range(count)]


def attend(query, keys, values, valid):
    width, size = query.shape
    team = len(keys)
    heads = width // HEAD_DIM
    span = team * size
    row_spec = pl.BlockSpec((1, 1, size), lambda head, *_: (head, 0, 0))
    return pl.pallas_call(
        functools.partial(attend_kernel, team),
        out_shape=(
            jax.ShapeDtypeStruct((width, size), jnp.bfloat16),
            jax.ShapeDtypeStruct((heads, 1, size), jnp.float32),
        ),
        grid_spec=pltpu.PrefetchScalarGridSpec(
            num_scalar_prefetch=1,
            grid=(heads,),
            in_specs=head_specs(size, 1 + 2 * team),
            out_specs=(head_specs(size, 1)[0], row_spec),
            scratch_shapes=[
                pltpu.VMEM((span, 2 * HEAD_DIM + SPARE), jnp.bfloat16),
                pltpu.VMEM((HEAD_DIM + SPARE, span), jnp.bfloat16),
            ],
        ),
        cost_estimate=pl.CostEstimate(
            flops=4 * width * size * span,
            bytes_accessed=2 * width * size * (2 + 2 * team),
            transcendentals=heads * size * span,
        ),
        name="attend",
    )(valid, query, *keys, *values)


def attend_back(query, out, grad, logs, keys, values, valid):
    width, size = query.shape
    team = len(keys)
    heads = width // HEAD_DIM
    span = team * size
    row_spec = pl.BlockSpec((1, 1, size), lambda head, *_: (head, 0, 0))
    shape = jax.ShapeDtypeStruct((width, size), jnp.bfloat16)
    results = pl.pallas_call(
        functools.partial(attend_back_kernel, team),
        out_shape=(shape,) * (1 + 2 * team),
        grid_spec=pltpu.PrefetchScalarGridSpec(
            num_scalar_prefetch=1,
            grid=(heads,),
            in_specs=head_specs(size, 3) + [row_spec] + head_specs(size, 2 * team),
            out_specs=head_specs(size, 1 + 2 * team),
            scratch_shapes=[
                pltpu.VMEM((span, 2 * HEAD_DIM + SPARE), jnp.bfloat16),
                pltpu.VMEM((span, HEAD_DIM + SPARE), jnp.bfloat16),
                pltpu.VMEM((HEAD_DIM, span), jnp.bfloat16),
                pltpu.VMEM((span, HEAD_DIM), jnp.float32),
                pltpu.VMEM((span, HEAD_DIM), jnp.float32),
            ],
        ),
        cost_estimate=pl.CostEstimate(
            flops=10 * width * size * span,
            bytes_accessed=2 * width * size * (4 + 4 * team),
            transcendentals=heads * size * span,
        ),
        name="attend_back",
    )(valid, query, out, grad, logs, *keys, *values)
    return results[0], results[1 : 1 + team], results[1 + team :]


def normalize(values):
    average = jnp.mean(values, axis=0, keepdims=True)
    inverse = lax.rsqrt(jnp.mean(values * values, axis=0, keepdims=True) - average * average + EPS)
    return ((values - average) * inverse, inverse)


def normalize_back(incoming, normed, inverse, gain):
    scaled = incoming * gain[:, None]
    total = jnp.mean(scaled, axis=0, keepdims=True)
    crossed = jnp.mean(scaled * normed, axis=0, keepdims=True)
    outgoing = inverse * (scaled - total - normed * crossed)
    return (outgoing, jnp.sum(incoming * normed, axis=1))


def gelu_parts(values):
    inside = 0.5 + 0.5 * lax.erf(values * math.sqrt(0.5))
    density = jnp.exp(-0.5 * values * values) * (1.0 / math.sqrt(2.0 * math.pi))
    return values * inside, inside + values * density


def product(spec, former, latter, kind=jnp.float32):
    return jnp.einsum(spec, former, latter, preferred_element_type=jnp.float32).astype(kind)


def update(weight, moment, average, gradient, rate):
    moment_next = MOMENTUM * moment + gradient
    weight_next = weight - rate * (gradient + MOMENTUM * moment_next)
    average_next = AVERAGING * average + (1.0 - AVERAGING) * weight_next
    return (moment_next, weight_next, average_next)


def gather_weight(shard, depth):
    whole = lax.all_gather(shard, EVERY, axis=0, tiled=True)
    return whole.reshape(depth, whole.shape[0] // depth, shard.shape[1])


def scatter_grad(parts):
    depth, width, columns = parts.shape
    return lax.psum_scatter(
        parts.reshape(depth * width, columns), EVERY, scatter_dimension=0, tiled=True
    ).astype(jnp.float32)


def on_device(
    inputs,
    cotangent,
    clip_lengths,
    project_weight,
    project_moment,
    project_average,
    output_weight,
    output_moment,
    output_average,
    expand_weight,
    expand_moment,
    expand_average,
    reduce_weight,
    reduce_moment,
    reduce_average,
    gain_first,
    first_moment,
    first_average,
    gain_second,
    second_moment,
    second_average,
):
    block_width, rows_local = inputs.shape
    depth = lax.axis_size(COL)
    team = depth // 2
    rows_of_weight = project_weight.shape[1]
    width = block_width * depth
    size = rows_local // depth
    bf16 = jnp.bfloat16

    project_full = gather_weight(
        project_weight.astype(bf16).transpose(1, 0, 2).reshape(rows_of_weight, 3 * block_width),
        depth,
    )
    output_full = gather_weight(output_weight.astype(bf16).T, depth)
    expand_full = gather_weight(expand_weight.astype(bf16), depth)
    reduce_full = gather_weight(reduce_weight.astype(bf16).T, depth)
    gains = lax.all_gather(jnp.stack([gain_first, gain_second]), COL, axis=1, tiled=True)
    lengths = lax.all_gather(clip_lengths, "core", axis=0, tiled=True)

    clip = lax.axis_index("zhi")
    length = lax.dynamic_index_in_dim(lengths, clip, 0, False)
    slot = lax.axis_index(TEAM)
    valid = jnp.clip(
        jnp.stack([length - (slot ^ step) * size for step in range(team)]), 0, size
    ).astype(jnp.int32)
    token_mask = (jnp.arange(size, dtype=jnp.int32) < valid[0]).astype(jnp.float32)[None, :]

    resident = to_tokens(inputs, depth).astype(jnp.float32)
    normed_one, inverse_one = normalize(resident)
    hidden_one = (normed_one * gains[0][:, None]).astype(bf16)
    projected = product(
        "zdke,dt->kzet",
        project_full.reshape(depth, width, 3, block_width),
        hidden_one,
        bf16,
    ).reshape(3, width, size)
    query = projected[0]
    both = projected[1:]
    others = [exchange(both, TEAM, step, team) for step in range(1, team)]
    keys = [both[0]] + [other[0] for other in others]
    values = [both[1]] + [other[1] for other in others]
    attended, logs = attend(query, keys, values, valid)
    middle = resident + product(
        "zde,zet->dt", output_full, attended.reshape(depth, block_width, size)
    )
    normed_two, inverse_two = normalize(middle)
    hidden_two = (normed_two * gains[1][:, None]).astype(bf16)
    pre_act = product("zdu,dt->zut", expand_full, hidden_two)
    activated, slope = gelu_parts(pre_act)
    activated, slope = activated.astype(bf16), slope.astype(bf16)
    block_output = to_features(
        (middle + product("zdu,zut->dt", reduce_full, activated)).astype(bf16), depth
    )

    upstream_low = to_tokens(cotangent, depth) * token_mask.astype(bf16)
    upstream = upstream_low.astype(jnp.float32)
    reduce_grad = scatter_grad(product("dt,zut->zdu", upstream_low, activated, bf16)).T
    pre_grad = (
        product("zdu,dt->zut", reduce_full, upstream_low) * slope.astype(jnp.float32)
    ).astype(bf16)
    expand_grad = scatter_grad(product("dt,zut->zdu", hidden_two, pre_grad, bf16))
    normed_two_grad = product("zdu,zut->dt", expand_full, pre_grad)
    middle_grad, gain_two_part = normalize_back(normed_two_grad, normed_two, inverse_two, gains[1])
    middle_grad = middle_grad + upstream
    middle_grad_low = middle_grad.astype(bf16)
    output_grad = scatter_grad(
        product(
            "dt,zet->zde", middle_grad_low, attended.reshape(depth, block_width, size), bf16
        )
    ).T
    attended_grad = product("zde,dt->zet", output_full, middle_grad_low, bf16).reshape(width, size)
    query_grad, key_grads, value_grads = attend_back(
        query, attended, attended_grad, logs, keys, values, valid
    )
    pair_grad = jnp.stack([key_grads[0], value_grads[0]]).astype(jnp.float32)
    for step in range(1, team):
        pair_grad = pair_grad + exchange(
            jnp.stack([key_grads[step], value_grads[step]]), TEAM, step, team
        ).astype(jnp.float32)
    stacked = jnp.concatenate([query_grad[None], pair_grad.astype(bf16)]).reshape(
        3, depth, block_width, size
    )
    project_grad = scatter_grad(
        product("dt,kzet->zdke", hidden_one, stacked, bf16).reshape(depth, width, 3 * block_width)
    )
    project_grad = project_grad.reshape(rows_of_weight, 3, block_width).transpose(1, 0, 2)
    normed_one_grad = product(
        "zdke,kzet->dt", project_full.reshape(depth, width, 3, block_width), stacked
    )
    input_grad, gain_one_part = normalize_back(normed_one_grad, normed_one, inverse_one, gains[0])
    input_grad = to_features((input_grad + middle_grad).astype(bf16), depth).astype(jnp.float32)
    gain_grads = lax.psum_scatter(
        lax.psum(jnp.stack([gain_one_part, gain_two_part]), ROW), COL, scatter_dimension=1, tiled=True
    )
    gain_one_grad, gain_two_grad = gain_grads[0], gain_grads[1]

    scale = 1.0 / math.sqrt(rows_local * lax.axis_size(ROW))
    pm, pw, pa = update(
        project_weight, project_moment, project_average, project_grad, RATE_PROJECT * scale
    )
    om, ow, oa = update(
        output_weight, output_moment, output_average, output_grad, RATE_OUTPUT * scale
    )
    em, ew, ea = update(
        expand_weight, expand_moment, expand_average, expand_grad, RATE_EXPAND * scale
    )
    rm, rw, ra = update(
        reduce_weight, reduce_moment, reduce_average, reduce_grad, RATE_REDUCE * scale
    )
    fm, fw, fa = update(gain_first, first_moment, first_average, gain_one_grad, RATE_GAIN * scale)
    sm, sw, sa = update(
        gain_second, second_moment, second_average, gain_two_grad, RATE_GAIN * scale
    )
    return (
        block_output,
        input_grad,
        project_grad,
        pm,
        pw,
        pa,
        pw.astype(bf16),
        output_grad,
        om,
        ow,
        oa,
        ow.astype(bf16),
        expand_grad,
        em,
        ew,
        ea,
        ew.astype(bf16),
        reduce_grad,
        rm,
        rw,
        ra,
        rw.astype(bf16),
        gain_one_grad,
        fm,
        fw,
        fa,
        gain_two_grad,
        sm,
        sw,
        sa,
    )


def solution(mesh):
    rows, columns = mesh.shape["row"], mesh.shape["col"]
    finer = Mesh(
        mesh.devices.reshape(rows // 2, 2, CLIPS_PER_COLUMN, columns // CLIPS_PER_COLUMN),
        ("pair", "core", "zhi", "zlo"),
    )
    plane = P(COL, ROW)
    weights = (P(None, ROW, COL), plane, P(ROW, COL), plane)
    placed = (plane, plane, P(ROW))
    for spec in weights:
        placed += (spec,) * 3
    placed += (P(COL),) * 6
    results = (plane, plane)
    for spec in weights:
        results += (spec,) * 5
    results += (P(COL),) * 8
    return jax.shard_map(
        on_device, mesh=finer, in_specs=placed, out_specs=results, check_vma=False
    )
```

time: 1830 us -> 1230 us (0.67)
  waiting for transfers between devices: 1040 us -> 548 us
  matrix products: 338 us -> 166 us
  Pallas kernels: 0 us -> 109 us
  other arithmetic: 122 us -> 38.9 us
  starting transfers between devices: 1.34 us -> 43.6 us
  loops' own time: 24.3 us -> 0 us
    all_gather x7 -> x4, waiting for transfers between devices: 545 us -> 106 us  [gather_weight(): whole = lax.all_gather(shard, EVERY, axis=0, tiled=True)]
    dot_general x54 -> x12, matrix products: 338 us -> 166 us  [product(): jnp.einsum(spec, former, latter, preferred_element_type=jnp.float32)]
    reduce_scatter x7 -> x3, waiting for transfers between devices: 492 us -> 339 us  [scatter_grad(): lax.psum_scatter(parts.reshape(depth * width, columns), EVERY, scatter_di...]
    pallas_call x0 -> x2, Pallas kernels: none -> 109 us  [the longest x1 60.4 us: attend_back(): pl.pallas_call(functools.partial(attend_back_kernel, team), out_shape=(sh...]
    ppermute x0 -> x18, waiting for transfers between devices: none -> 102 us  [the longest x8 76.1 us: to_features(): piece = lax.ppermute(chunk, COLUMN, back)]
    all_gather x1, blocking collectives: 16.3 us -> 97.5 us  [on_device(): lax.all_gather(jnp.stack([gain_first, gain_second]), COL, axis=1, tiled=T...]
    psum x5 -> x1, blocking collectives: 84.3 us -> 12 us  [on_device(): lax.psum(jnp.stack([gain_one_part, gain_two_part]), ROW)]
    convert_element_type x20 -> x9, other arithmetic: 61.1 us -> 16.7 us  [the longest x1 3.25 us: on_device(): pair_grad.astype(bf16)]
  transfers between devices with their start and end apart: 15 -> 27, of which waited for: 11 -> 11; matrix products, arithmetic and copies ran while one was open for 22% -> 22% of each run, Pallas kernels for 0% -> 4%
where the time goes in v1:
time: 1230 us; the launch traced here: 1210 us
  waiting for transfers between devices  548 us (45%)
  local copies, waits for them, and re-layouts  173 us (14%)
  matrix products  166 us (13%)
  blocking collectives  115 us (9%)
  Pallas kernels  109 us (9%)
  starting transfers between devices  43.6 us (4%)
  other arithmetic  38.9 us (3%)
  between operations  17 us (1%)
    reduce_scatter x3, waiting for transfers between devices, scatter_grad(): lax.psum_scatter(parts.reshape(depth * width, columns), EVERY, scatter_di...  339 us
    dot_general x12, matrix products, product(): jnp.einsum(spec, former, latter, preferred_element_type=jnp.float32)  166 us
    all_gather x4, waiting for transfers between devices, gather_weight(): whole = lax.all_gather(shard, EVERY, axis=0, tiled=True)  106 us
    all_gather x1, blocking collectives, on_device(): lax.all_gather(jnp.stack([gain_first, gain_second]), COL, axis=1, tiled=T...  97.5 us
    ppermute x8, waiting for transfers between devices, to_features(): piece = lax.ppermute(chunk, COLUMN, back)  76.1 us
    unnamed x104, local copies, waits for them, and re-layouts  75.3 us
    pallas_call x1, Pallas kernels, attend_back(): pl.pallas_call(functools.partial(attend_back_kernel, team), out_shape=(sh...  60.4 us
    pallas_call x1, Pallas kernels, attend(): pl.pallas_call(functools.partial(attend_kernel, team), out_shape=(jax.Sha...  48.8 us
  transfers between devices with their start and end apart: 27, of which 11 were waited for; matrix products, arithmetic and copies ran while one was open for 22% of the time, Pallas kernels for 4%

profile of v1, /device:TPU:8, one launch (start us, length us, event | category | flops | bytes accessed | tf_op | source)
XLA Modules:
  0.0 1211.0 jit_solution(9717985378712194480)
XLA Ops:
  26.2 9.3 collective-permute-start.2
  35.5 8.4 collective-permute-done.11
  47.7 11.0 collective-permute-done.10
  60.8 97.5 %all-gather = f32[4,320,2]{1,2,0:T(2,128)S(1)} all-gather(f32[1,320,2]{1,2,0:T(2,128)S(1)} %maximum_bitcast_fusion), channel_id=1, replica_groups=mesh['pair'=4,'core'=2,'zhi'=4,'zlo'=1] {'zhi','zlo'}, dimensions={0}, use_global_device_ids=true | all-gather | bytes 12800 | tf_op jit(solution)/shard_map/all_gather | solution.py:349
  174.9 13.7 %copy.186 = bf16[5120,960]{0,1:T(8,128)(2,1)} copy(bf16[5120,960]{1,0:T(8,128)(2,1)} %all-gather.6.cloned.1.call-done) | data formatting | bytes 19660800 | tf_op jit(solution)/shard_map/all_gather | solution.py:300
  188.6 18.3 %reshape_reshape.7 = bf16[4,1280,3,320]{1,0,3,2:T(4,128)(2,1)} reshape(bf16[5120,960]{0,1:T(8,128)(2,1)} %copy.186) | data formatting | bytes 19660800 | tf_op jit(solution)/shard_map/reshape;reshape | solution.py:365
  206.9 12.4 %convert_bitcast_fusion = bf16[3,4,320,768]{3,2,0,1:T(8,128)(2,1)S(1)} fusion(bf16[4,1280,3,320]{1,0,3,2:T(4,128)(2,1)} %reshape_reshape.7, bf16[1280,768]{0,1:T(8,128)(2,1)S(1)} %concatenate.14, f32[1280]{0:T(1024)S(1)} %get-tuple-element.145, f32[768]{0:T(1024)S(1)} %get-tuple-element.202, f32[768]{0:T(1024)S(1)} %get-tuple-element.201), kind=kOutput, calls=%fused_computation.28 | convolution fusion | flops 7557611520 | bytes 17705984 | tf_op jit(solution)/shard_map/zdke,dt->kzet/dot_general | solution.py:289
  225.6 6.0 all-reduce
  244.3 5.7 fusion.63
  254.5 48.8 %attend.1 = (bf16[1280,768]{1,0:T(8,128)(2,1)}, f32[16,1,768]{2,1,0:T(1,128)}) custom-call(s32[2]{0:T(128)} %copy-done.35, bf16[1280,768]{1,0:T(8,128)(2,1)} %bitcast.206, bf16[1280,768]{1,0:T(8,128)(2,1)} %bitcast.204, bf16[1280,768]{1,0:T(8,128)(2,1)} %get-tuple-element.172.refs_2_.refs_5_, bf16[1280,768]{1,0:T(8,128)(2,1)} %bitcast.202, ...), custom_call_target="tpu_custom_call" | custom-call | flops 6039797760 | bytes 11796480 | tf_op jit(solution)/shard_map/attend/pallas_call | solution.py:210
  303.4 8.4 fusion.58
  314.2 19.6 %fusion.9 = (bf16[4,1280,768]{1,2,0:T(8,128)(2,1)}, f32[768,4,1280]{2,0,1:T(8,128)}) fusion(bf16[4,1280,1280]{2,1,0:T(8,128)(2,1)} %bitcast.220, f32[1280,768]{0,1:T(8,128)} %get-tuple-element.203, f32[1280]{0:T(1024)S(1)} %get-tuple-element.144, f32[768]{0:T(1024)S(1)} %get-tuple-element.200, f32[768]{0:T(1024)S(1)} %get-tuple-element.199), kind=kOutput, calls=%fused_computation.15 | convolution fusion | flops 10089922560 | bytes 40643584 | tf_op jit(solution)/shard_map/zdu,dt->zut/dot_general | solution.py:289
  333.8 16.8 %convolution_convert_fusion = bf16[4,1280,1280]{1,2,0:T(8,128)(2,1)} fusion(bf16[4,1280,768]{1,2,0:T(8,128)(2,1)} %get-tuple-element.204, bf16[1280,768]{0,1:T(8,128)(2,1)S(1)} %copy-done.3, bf16[768]{0:T(1024)(128)(2,1)S(1)} %convert_convert_fusion), kind=kOutput, calls=%fused_computation | convolution fusion | flops 10073866240 | bytes 22939136 | tf_op jit(solution)/shard_map/dt,zut->zdu/dot_general | solution.py:289
  350.7 147.8 %reduce-scatter.14.cloned.1.call-done = bf16[160,1280]{1,0:T(8,128)(2,1)} async-done(((bf16[5120,1280]{1,0:T(8,128)(2,1)}), bf16[160,1280]{1,0:T(8,128)(2,1)}) %reduce-scatter.14.cloned.1.call-update) | async-done | bytes 409616 | tf_op jit(solution)/shard_map/reduce_scatter | solution.py:306
  501.7 103.7 %all-gather.12.cloned.1.call-done = bf16[5120,1280]{1,0:T(8,128)(2,1)} async-done(((bf16[160,1280]{1,0:T(8,128)(2,1)}), bf16[5120,1280]{1,0:T(8,128)(2,1)}) %all-gather.12.cloned.1.call-update) | async-done | bytes 13107216 | tf_op jit(solution)/shard_map/all_gather | solution.py:300
  605.4 19.0 %fusion.5 = bf16[4,1280,768]{1,2,0:T(8,128)(2,1)} fusion(bf16[4,1280,1280]{2,1,0:T(8,128)(2,1)} %bitcast.222, f32[768,4,1280]{2,0,1:T(8,128)} %get-tuple-element.205, bf16[1280,768]{0,1:T(8,128)(2,1)} %concatenate.15, bf16[768]{0:T(1024)(128)(2,1)S(1)} %convert_convert_fusion), kind=kOutput, calls=%fused_computation.9 | convolution fusion | flops 10117447680 | bytes 38667776 | tf_op jit(solution)/shard_map/zdu,dt->zut/dot_general | solution.py:289
  624.3 18.3 %fusion.29 = (f32[1280]{0:T(1024)S(1)}, f32[768]{0:T(1024)S(1)}, f32[768]{0:T(1024)S(1)}, f32[768,1280,1]{1,0,2:T(8,128)}) fusion(f32[1280,768]{0,1:T(8,128)} %get-tuple-element.203, f32[768]{0:T(1024)S(1)} %get-tuple-element.200, f32[768]{0:T(1024)S(1)} %get-tuple-element.199, f32[1280]{0:T(1024)S(1)} %get-tuple-element.144, ...), kind=kOutput, calls=%fused_computation.48 | convolution fusion | flops 10074190848 | bytes 28858368 | tf_op jit(solution)/shard_map/zdu,zut->dt/dot_general | solution.py:289
  651.2 60.4 %attend_back.1 = (bf16[1280,768]{1,0:T(8,128)(2,1)}, bf16[1280,768]{1,0:T(8,128)(2,1)}, bf16[1280,768]{1,0:T(8,128)(2,1)}, bf16[1280,768]{1,0:T(8,128)(2,1)}, bf16[1280,768]{1,0:T(8,128)(2,1)}) custom-call(s32[2]{0:T(128)} %copy-done.35, bf16[1280,768]{1,0:T(8,128)(2,1)} %bitcast.207, bf16[1280,768]{1,0:T(8,128)(2,1)} %get-tuple-element.37.refs_1_, ...), custom_call_target="tpu_custom_call" | custom-call | flops 15099494400 | bytes 23592960 | tf_op jit(solution)/shard_map/attend_back/pallas_call | solution.py:242
  714.6 6.5 collective-permute-done.13
  724.5 10.8 fusion.26
  736.5 7.1 fusion.30
  743.6 6.1 copy.250
  749.8 15.2 %fusion.14 = bf16[4,1280,3,320]{1,3,0,2:T(8,128)(2,1)} fusion(bf16[2,4,320,768]{3,2,1,0:T(8,128)(2,1)} %bitcast.192, bf16[1,4,320,768]{3,2,1,0:T(8,128)(2,1)} %bitcast.228, bf16[1280,768]{0,1:T(8,128)(2,1)S(1)} %concatenate.14, f32[1280]{0:T(1024)S(1)} %get-tuple-element.145, f32[768]{0:T(1024)S(1)} %get-tuple-element.202, f32[768]{0:T(1024)S(1)} %get-tuple-element.201), kind=kOutput, calls=%fused_computation.21 | convolution fusion | flops 7562526720 | bytes 17705984 | tf_op jit(solution)/shard_map/dt,kzet->zdke/dot_general | solution.py:289
  765.0 23.3 %copy.249 = bf16[4,1280,3,320]{3,2,1,0:T(4,128)(2,1)} copy(bf16[4,1280,3,320]{1,3,0,2:T(8,128)(2,1)} %fusion.14) | data formatting | bytes 19660800
  788.3 29.7 %reshape.195 = bf16[5120,960]{1,0:T(8,128)(2,1)} reshape(bf16[4,1280,3,320]{3,2,1,0:T(4,128)(2,1)} %copy.249) | data formatting | bytes 19660800
  818.0 17.1 %convolution_convert_fusion.1 = bf16[4,1280,1280]{1,2,0:T(8,128)(2,1)} fusion(bf16[4,1280,768]{1,2,0:T(8,128)(2,1)} %fusion.5, f32[1280,768]{0,1:T(8,128)} %get-tuple-element.203, f32[1280]{0:T(1024)S(1)} %get-tuple-element.144, f32[768]{0:T(1024)S(1)} %get-tuple-element.200, f32[768]{0:T(1024)S(1)} %get-tuple-element.199), kind=kOutput, calls=%fused_computation.1 | convolution fusion | flops 10076815360 | bytes 24914944 | tf_op jit(solution)/shard_map/dt,zut->zdu/dot_general | solution.py:289
  838.7 16.8 %fusion.28 = bf16[1280,768]{0,1:T(8,128)(2,1)S(1)} fusion(f32[1280,768]{0,1:T(8,128)} %get-tuple-element.203, bf16[4,1280,768]{1,2,0:T(8,128)(2,1)} %get-tuple-element.204, bf16[4,1280,1280]{2,1,0:T(8,128)(2,1)} %bitcast.223), kind=kOutput, calls=%fused_computation.45 | convolution fusion | flops 10068295680 | bytes 26869760 | tf_op jit(solution)/shard_map/zdu,zut->dt/dot_general | solution.py:289
  879.4 42.7 %collective-permute-done.6 = bf16[320,768]{1,0:T(8,128)(2,1)} collective-permute-done((bf16[320,768]{1,0:T(8,128)(2,1)}, bf16[320,768]{1,0:T(8,128)(2,1)}, u32[]{:S(2)}, u32[]{:S(2)}) %collective-permute-start.6) | collective-permute-done | bytes 491552 | tf_op jit(solution)/shard_map/ppermute | solution.py:84
  944.4 12.0 psum.8
  964.3 31.0 %collective-permute-done.15 = bf16[320,768]{1,0:T(8,128)(2,1)} collective-permute-done((bf16[320,768]{1,0:T(8,128)(2,1)}, bf16[320,768]{1,0:T(8,128)(2,1)}, u32[]{:S(2)}, u32[]{:S(2)}) %collective-permute-start.15) | collective-permute-done | bytes 491552 | tf_op jit(solution)/shard_map/ppermute | solution.py:84
  1001.1 38.0 %reduce-scatter.16.cloned.1.call-done = bf16[160,960]{1,0:T(8,128)(2,1)} async-done(((bf16[5120,960]{1,0:T(8,128)(2,1)}), bf16[160,960]{1,0:T(8,128)(2,1)}) %reduce-scatter.16.cloned.1.call-update) | async-done | bytes 307216 | tf_op jit(solution)/shard_map/reduce_scatter | solution.py:306
  1045.5 153.5 %reduce-scatter.12.cloned.1.call-done = bf16[160,1280]{1,0:T(8,128)(2,1)} async-done(((bf16[5120,1280]{1,0:T(8,128)(2,1)}), bf16[160,1280]{1,0:T(8,128)(2,1)}) %reduce-scatter.12.cloned.1.call-update) | async-done | bytes 409616 | tf_op jit(solution)/shard_map/reduce_scatter | solution.py:306
  (235 shorter events, 158.9 us)
Async XLA Ops:
  7.2 167.7 %all-gather.6.cloned.1.call-start = ((), (), s32[]{:S(2)}) async-start(), calls=%async_computation.5 | async-start | bytes 10813440 | tf_op jit(solution)/shard_map/all_gather | solution.py:300
  9.8 293.5 %all-gather.8.cloned.1.call-start = ((), (), s32[]{:S(2)}) async-start(), calls=%async_computation.6 | async-start | bytes 4055040 | tf_op jit(solution)/shard_map/all_gather | solution.py:300
  11.5 302.6 %all-gather.10.cloned.1.call-start = ((), (), s32[]{:S(2)}) async-start(), calls=%async_computation.7 | async-start | bytes 13516800 | tf_op jit(solution)/shard_map/all_gather | solution.py:300
  12.4 486.1 %reduce-scatter.14.cloned.1.call-start = ((), (), s32[]{:S(2)}) async-start(), calls=%async_computation.10 | async-start | bytes 13516800 | tf_op jit(solution)/shard_map/reduce_scatter | solution.py:306
  14.1 12.1 collective-permute-start.12
  14.8 29.1 %collective-permute-start.11 = (bf16[320,768]{1,0:T(8,128)(2,1)S(1)}, bf16[320,768]{1,0:T(8,128)(2,1)S(1)}, u32[]{:S(2)}, u32[]{:S(2)}) collective-permute-start(bf16[320,768]{1,0:T(8,128)(2,1)S(1)} %get-tuple-element.184), channel_id=1, source_target_pairs={{0,1},{1,5},{2,0},{3,4},{4,3},{5,7},{6,2},{7,6},{8,9},{9,13},{10,8... | collective-permute-start | bytes 1474568 | tf_op jit(solution)/shard_map/ppermute | solution.py:69
  18.8 39.9 %collective-permute-start.10 = (bf16[320,768]{1,0:T(8,128)(2,1)S(1)}, bf16[320,768]{1,0:T(8,128)(2,1)S(1)}, u32[]{:S(2)}, u32[]{:S(2)}) collective-permute-start(bf16[320,768]{1,0:T(8,128)(2,1)S(1)} %get-tuple-element.182), channel_id=1, source_target_pairs={{0,4},{1,0},{2,5},{3,1},{4,6},{5,2},{6,7},{7,3},{8,12},{9,8},{10,1... | collective-permute-start | bytes 1474568 | tf_op jit(solution)/shard_map/ppermute | solution.py:69
  18.8 139.6 %collective-permute-start.9 = (bf16[320,768]{1,0:T(8,128)(2,1)S(1)}, bf16[320,768]{1,0:T(8,128)(2,1)S(1)}, u32[]{:S(2)}, u32[]{:S(2)}) collective-permute-start(bf16[320,768]{1,0:T(8,128)(2,1)S(1)} %get-tuple-element.181), channel_id=1, source_target_pairs={{0,0},{1,4},{2,1},{3,5},{4,2},{5,6},{6,3},{7,7},{8,8},{9,12},{10,9... | collective-permute-start | bytes 1474568 | tf_op jit(solution)/shard_map/ppermute | solution.py:69
  24.5 136.3 %collective-permute-start.3 = (bf16[320,768]{1,0:T(8,128)(2,1)}, bf16[320,768]{1,0:T(8,128)(2,1)S(1)}, u32[]{:S(2)}, u32[]{:S(2)}) collective-permute-start(bf16[320,768]{1,0:T(8,128)(2,1)} %get-tuple-element.195), channel_id=1, source_target_pairs={{0,5},{1,1},{2,4},{3,0},{4,7},{5,3},{6,6},{7,2},{8,13},{9,9},{10,1... | collective-permute-start | bytes 1474568 | tf_op jit(solution)/shard_map/ppermute | solution.py:69
  26.2 134.6 %collective-permute-start.2 = (bf16[320,768]{1,0:T(8,128)(2,1)}, bf16[320,768]{1,0:T(8,128)(2,1)}, u32[]{:S(2)}, u32[]{:S(2)}) collective-permute-start(bf16[320,768]{1,0:T(8,128)(2,1)} %get-tuple-element.196), channel_id=1, source_target_pairs={{0,1},{1,5},{2,0},{3,4},{4,3},{5,7},{6,2},{7,6},{8,9},{9,13},{10,8... | collective-permute-start | bytes 1474568 | tf_op jit(solution)/shard_map/ppermute | solution.py:69
  43.9 114.6 %copy-start.20 = (bf16[320,768]{1,0:T(8,128)(2,1)}, bf16[320,768]{1,0:T(8,128)(2,1)S(1)}, u32[]{:S(2)}) copy-start(bf16[320,768]{1,0:T(8,128)(2,1)S(1)} %collective-permute-done.11) | copy-start | bytes 1474564
  43.9 116.9 %collective-permute-start.1 = (bf16[320,768]{1,0:T(8,128)(2,1)}, bf16[320,768]{1,0:T(8,128)(2,1)}, u32[]{:S(2)}, u32[]{:S(2)}) collective-permute-start(bf16[320,768]{1,0:T(8,128)(2,1)} %get-tuple-element.194), channel_id=1, source_target_pairs={{0,4},{1,0},{2,5},{3,1},{4,6},{5,2},{6,7},{7,3},{8,12},{9,8},{10,1... | collective-permute-start | bytes 1474568 | tf_op jit(solution)/shard_map/ppermute | solution.py:69
  58.7 99.7 %copy-start.21 = (bf16[320,768]{1,0:T(8,128)(2,1)}, bf16[320,768]{1,0:T(8,128)(2,1)S(1)}, u32[]{:S(2)}) copy-start(bf16[320,768]{1,0:T(8,128)(2,1)S(1)} %collective-permute-done.10) | copy-start | bytes 1474564
  58.7 102.1 %collective-permute-start = (bf16[320,768]{1,0:T(8,128)(2,1)S(1)}, bf16[320,768]{1,0:T(8,128)(2,1)}, u32[]{:S(2)}, u32[]{:S(2)}) collective-permute-start(bf16[320,768]{1,0:T(8,128)(2,1)S(1)} %get-tuple-element.193), channel_id=1, source_target_pairs={{0,0},{1,4},{2,1},{3,5},{4,2},{5,6},{6,3},{7,7},{8,8},{9,12},{10,9... | collective-permute-start | bytes 1474568 | tf_op jit(solution)/shard_map/ppermute | solution.py:69
  224.1 26.0 %collective-permute-start.4 = (bf16[2,1280,768]{2,1,0:T(8,128)(2,1)}, bf16[2,1280,768]{2,1,0:T(8,128)(2,1)}, u32[]{:S(2)}, u32[]{:S(2)}) collective-permute-start(bf16[2,1280,768]{2,1,0:T(8,128)(2,1)} %bitcast.20), channel_id=1, source_target_pairs={{0,4},{4,0},{1,5},{5,1},{2,6},{6,2},{3,7},{7,3},{8,12},{12,8},{9,1... | collective-permute-start | bytes 11796488 | tf_op jit(solution)/shard_map/ppermute | solution.py:35
  350.6 147.9 %copy-start.19 = (f32[1280,160]{0,1:T(8,128)S(1)}, f32[1280,160]{0,1:T(8,128)}, u32[]{:S(2)}) copy-start(f32[1280,160]{0,1:T(8,128)} %param.33) | copy-start | bytes 2457604
  350.7 254.7 %all-gather.12.cloned.1.call-start = ((), (), s32[]{:S(2)}) async-start(), calls=%async_computation.8 | async-start | bytes 13516800 | tf_op jit(solution)/shard_map/all_gather | solution.py:300
  501.6 441.8 %reduce-scatter.20.cloned.1.call-start = ((), (), s32[]{:S(2)}) async-start(), calls=%async_computation.13 | async-start | bytes 819200
  714.3 6.8 collective-permute-start.13
  736.5 221.2 %reduce-scatter.18.cloned.1.call-start = ((), (), s32[]{:S(2)}) async-start(), calls=%async_computation.12 | async-start | bytes 4055040
  749.7 289.3 %reduce-scatter.16.cloned.1.call-start = ((), (), s32[]{:S(2)}) async-start(), calls=%async_computation.11 | async-start | bytes 10813440 | tf_op jit(solution)/shard_map/reduce_scatter | solution.py:306
  818.0 381.1 %reduce-scatter.12.cloned.1.call-start = ((), (), s32[]{:S(2)}) async-start(), calls=%async_computation.9 | async-start | bytes 13516800 | tf_op jit(solution)/shard_map/reduce_scatter | solution.py:306
  860.1 17.9 %collective-permute-start.5 = (bf16[320,768]{1,0:T(8,128)(2,1)}, bf16[320,768]{1,0:T(8,128)(2,1)}, u32[]{:S(2)}, u32[]{:S(2)}) collective-permute-start(bf16[320,768]{1,0:T(8,128)(2,1)} %copy.192), channel_id=1, source_target_pairs={{0,0},{4,1},{1,2},{5,3},{2,4},{6,5},{3,6},{7,7},{8,8},{12,9},{9,10... | collective-permute-start | bytes 1474568 | tf_op jit(solution)/shard_map/ppermute | solution.py:84
  865.3 56.8 %collective-permute-start.6 = (bf16[320,768]{1,0:T(8,128)(2,1)}, bf16[320,768]{1,0:T(8,128)(2,1)}, u32[]{:S(2)}, u32[]{:S(2)}) collective-permute-start(bf16[320,768]{1,0:T(8,128)(2,1)} %copy.193), channel_id=1, source_target_pairs={{4,0},{0,1},{5,2},{1,3},{6,4},{2,5},{7,6},{3,7},{12,8},{8,9},{13,1... | collective-permute-start | bytes 1474568 | tf_op jit(solution)/shard_map/ppermute | solution.py:84
  868.7 54.5 %collective-permute-start.7 = (bf16[320,768]{1,0:T(8,128)(2,1)}, bf16[320,768]{1,0:T(8,128)(2,1)}, u32[]{:S(2)}, u32[]{:S(2)}) collective-permute-start(bf16[320,768]{1,0:T(8,128)(2,1)} %copy.194), channel_id=1, source_target_pairs={{1,0},{5,1},{0,2},{4,3},{3,4},{7,5},{2,6},{6,7},{9,8},{13,9},{8,10... | collective-permute-start | bytes 1474568 | tf_op jit(solution)/shard_map/ppermute | solution.py:84
  871.6 52.7 %collective-permute-start.8 = (bf16[320,768]{1,0:T(8,128)(2,1)}, bf16[320,768]{1,0:T(8,128)(2,1)S(1)}, u32[]{:S(2)}, u32[]{:S(2)}) collective-permute-start(bf16[320,768]{1,0:T(8,128)(2,1)} %copy.195), channel_id=1, source_target_pairs={{5,0},{1,1},{4,2},{0,3},{7,4},{3,5},{6,6},{2,7},{13,8},{9,9},{12,1... | collective-permute-start | bytes 1474568 | tf_op jit(solution)/shard_map/ppermute | solution.py:84
  929.8 33.2 %collective-permute-start.14 = (bf16[320,768]{1,0:T(8,128)(2,1)}, bf16[320,768]{1,0:T(8,128)(2,1)}, u32[]{:S(2)}, u32[]{:S(2)}) collective-permute-start(bf16[320,768]{1,0:T(8,128)(2,1)} %copy.203), channel_id=1, source_target_pairs={{0,0},{4,1},{1,2},{5,3},{2,4},{6,5},{3,6},{7,7},{8,8},{12,9},{9,10... | collective-permute-start | bytes 1474568 | tf_op jit(solution)/shard_map/ppermute | solution.py:84
  933.8 61.5 %collective-permute-start.15 = (bf16[320,768]{1,0:T(8,128)(2,1)}, bf16[320,768]{1,0:T(8,128)(2,1)}, u32[]{:S(2)}, u32[]{:S(2)}) collective-permute-start(bf16[320,768]{1,0:T(8,128)(2,1)} %copy.204), channel_id=1, source_target_pairs={{4,0},{0,1},{5,2},{1,3},{6,4},{2,5},{7,6},{3,7},{12,8},{8,9},{13,1... | collective-permute-start | bytes 1474568 | tf_op jit(solution)/shard_map/ppermute | solution.py:84
  937.1 59.3 %collective-permute-start.16 = (bf16[320,768]{1,0:T(8,128)(2,1)}, bf16[320,768]{1,0:T(8,128)(2,1)}, u32[]{:S(2)}, u32[]{:S(2)}) collective-permute-start(bf16[320,768]{1,0:T(8,128)(2,1)} %copy.205), channel_id=1, source_target_pairs={{1,0},{5,1},{0,2},{4,3},{3,4},{7,5},{2,6},{6,7},{9,8},{13,9},{8,10... | collective-permute-start | bytes 1474568 | tf_op jit(solution)/shard_map/ppermute | solution.py:84
  938.1 59.4 %collective-permute-start.17 = (bf16[320,768]{1,0:T(8,128)(2,1)}, bf16[320,768]{1,0:T(8,128)(2,1)}, u32[]{:S(2)}, u32[]{:S(2)}) collective-permute-start(bf16[320,768]{1,0:T(8,128)(2,1)} %copy.206), channel_id=1, source_target_pairs={{5,0},{1,1},{4,2},{0,3},{7,4},{3,5},{6,6},{2,7},{13,8},{9,9},{12,1... | collective-permute-start | bytes 1474568 | tf_op jit(solution)/shard_map/ppermute | solution.py:84
  1040.6 158.5 %copy-start.8 = (f32[160,1280]{1,0:T(8,128)S(1)}, f32[160,1280]{1,0:T(8,128)}, u32[]{:S(2)}) copy-start(f32[160,1280]{1,0:T(8,128)} %param.30) | copy-start | bytes 2457604
  1043.2 161.1 %copy-start.12 = (f32[3,160,320]{2,1,0:T(8,128)}, f32[3,160,320]{2,1,0:T(8,128)S(1)}, u32[]{:S(2)}) copy-start(f32[3,160,320]{2,1,0:T(8,128)S(1)} %get-tuple-element.165) | copy-start | bytes 1843204
  (38 other events, 678.5 us)
Sparse Core Ops, SparseCore 0:
  11.4 134.4 all-gather.5
  149.4 64.5 all-gather.7
  217.4 96.7 all-gather.9
  350.8 147.6 reduce-scatter.13
  501.8 103.5 all-gather.11
  736.6 19.0 reduce-scatter.19
  761.0 105.3 reduce-scatter.17
  868.7 170.2 reduce-scatter.15
  1041.4 157.6 reduce-scatter.11

commit v2 on v1

--- a/solution.py
+++ b/solution.py
@@ -86,9 +86,609 @@
     return whole
 
 
+MESH_ID = pl.DeviceIdType.MESH
+
+
+def places():
+    return (
+        lax.axis_index("pair"),
+        lax.axis_index("core"),
+        lax.axis_index("zhi"),
+    )
+
+
+def device(pair, core, place):
+    return (pair, core, place, 0)
+
+
+def greet(pair, core, place):
+    barrier = pltpu.get_barrier_semaphore()
+    others = [device(pair ^ 1, core, place), device(pair ^ 2, core, place)]
+    for flip in range(2):
+        for step in range(CLIPS_PER_COLUMN):
+            if flip or step:
+                others.append(device(pair, core ^ flip, place ^ step))
+    for other in others:
+        pl.semaphore_signal(barrier, inc=1, device_id=other, device_id_type=MESH_ID)
+    pl.semaphore_wait(barrier, len(others))
+
+
+def gather_kernel(groups, values_ref, gain_ref, *refs):
+    shards, wholes = refs[:groups], refs[groups + 2 : 2 * groups + 2]
+    tokens_ref, gains_ref = refs[groups : groups + 2]
+    (x_send, x_recv, g_send, g_recv, own_sem, z_send, z_recv, p_send, p_recv, c_send, c_recv) = (
+        refs[2 * groups + 2 :]
+    )
+    pair, core, place = places()
+    row = 2 * pair + core
+    depth = CLIPS_PER_COLUMN
+    block, rows = values_ref.shape
+    size = rows // depth
+    greet(pair, core, place)
+
+    def remote(source, target, send, recv, where):
+        return pltpu.make_async_remote_copy(
+            src_ref=source,
+            dst_ref=target,
+            send_sem=send,
+            recv_sem=recv,
+            device_id=where,
+            device_id_type=MESH_ID,
+        )
+
+    mine = (place % 2) * 2 + core
+    targets = []
+    for step in range(depth):
+        chunk = place ^ step
+        to_core, to_place = chunk % 2, 2 * core + chunk // 2
+        source = values_ref.at[:, pl.ds(pl.multiple_of(chunk * size, size), size)]
+        home = tokens_ref.at[place]
+        away = (to_core != core) | (to_place != place)
+        copy = remote(
+            source, home, x_send.at[step], x_recv.at[step], device(pair, to_core, to_place)
+        )
+        local = pltpu.make_async_copy(source, home, x_recv.at[step])
+        targets.append((away, copy, local))
+
+        @pl.when(away)
+        def _():
+            copy.start()
+
+        @pl.when(jnp.logical_not(away))
+        def _():
+            local.start()
+
+    def piece(group, step, other, flip):
+        return wholes[group].at[place ^ step, 2 * (pair ^ other) + (core ^ flip)]
+
+    own = [
+        pltpu.make_async_copy(shards[group], piece(group, 0, 0, 0), own_sem.at[group])
+        for group in range(groups)
+    ]
+    sends = []
+    own.append(pltpu.make_async_copy(gain_ref, gains_ref.at[place], g_recv.at[0]))
+    for step in range(1, depth):
+        copy = remote(
+            gain_ref,
+            gains_ref.at[place],
+            g_send.at[step],
+            g_recv.at[step],
+            device(pair, core, place ^ step),
+        )
+        copy.start()
+        sends.append(copy)
+    for group in range(groups):
+        for step in range(1, depth):
+            copy = remote(
+                shards[group],
+                wholes[group].at[place, row],
+                z_send.at[group, step],
+                z_recv.at[group, step],
+                device(pair, core, place ^ step),
+            )
+            copy.start()
+            sends.append(copy)
+    for copy in own:
+        copy.start()
+
+    def to_pair(group, step, other, hop, slot):
+        source = (
+            shards[group] if step == 0 and other == 0 else piece(group, step, other, 0)
+        )
+        copy = remote(
+            source,
+            piece(group, step, other, 0),
+            p_send.at[group, step, slot],
+            p_recv.at[group, step, other ^ hop],
+            device(pair ^ hop, core, place),
+        )
+        copy.start()
+        sends.append(copy)
+
+    def to_core(group, step, other):
+        source = (
+            shards[group] if step == 0 and other == 0 else piece(group, step, other, 0)
+        )
+        copy = remote(
+            source,
+            piece(group, step, other, 0),
+            c_send.at[group, step, other],
+            c_recv.at[group, step, other],
+            device(pair, core ^ 1, place),
+        )
+        copy.start()
+        sends.append(copy)
+
+    def await_piece(group, step, other, flip, sem):
+        here = piece(group, step, other, flip)
+        remote(here, here, sem, sem, device(pair ^ 1, core, place)).wait_recv()
+
+    order = [(group, step) for step in range(depth) for group in range(groups)]
+
+    def first_hop(group, step):
+        if step:
+            await_piece(group, step, 0, 0, z_recv.at[group, step])
+        near, far = (1, 2) if (group + step) % 2 == 0 else (2, 1)
+        to_pair(group, step, 0, near, 0)
+        to_pair(group, step, 0, far, 1)
+        to_core(group, step, 0)
+
+    def second_hop(group, step):
+        near, far = (1, 2) if (group + step) % 2 == 0 else (2, 1)
+        await_piece(group, step, near, 0, p_recv.at[group, step, near])
+        to_pair(group, step, near, far, 2)
+        to_core(group, step, near)
+
+    def last_hop(group, step):
+        near, far = (1, 2) if (group + step) % 2 == 0 else (2, 1)
+        for other in (far, 3):
+            await_piece(group, step, other, 0, p_recv.at[group, step, other])
+            to_core(group, step, other)
+
+    for at in range(len(order) + 4):
+        if at < len(order):
+            first_hop(*order[at])
+        if 0 <= at - 2 < len(order):
+            second_hop(*order[at - 2])
+        if 0 <= at - 4:
+            last_hop(*order[at - 4])
+    for group, step in order:
+        for other in range(4):
+            await_piece(group, step, other, 1, c_recv.at[group, step, other])
+    for step in range(1, depth):
+        here = gains_ref.at[place ^ step]
+        remote(
+            here, here, g_recv.at[step], g_recv.at[step], device(pair, core ^ 1, place)
+        ).wait_recv()
+    for copy in own:
+        copy.wait()
+    for copy in sends:
+        copy.wait_send()
+    for step in range(depth):
+        away, copy, local = targets[step]
+        home = tokens_ref.at[place]
+        from_core, from_place = place // 2, mine ^ step
+        foreign = (from_core != core) | (from_place != place)
+
+        @pl.when(foreign)
+        def _():
+            remote(
+                home, home, x_recv.at[step], x_recv.at[step], device(pair, core ^ 1, place)
+            ).wait_recv()
+
+        @pl.when(jnp.logical_not(foreign))
+        def _():
+            pltpu.make_async_copy(home, home, x_recv.at[step]).wait()
+
+        @pl.when(away)
+        def _():
+            copy.wait_send()
+
+
+def gather_all(values, gain, shards):
+    groups = len(shards)
+    depth = CLIPS_PER_COLUMN
+    block, rows = values.shape
+    size = rows // depth
+    dma = pltpu.SemaphoreType.DMA
+    anywhere = pl.BlockSpec(memory_space=pl.ANY)
+    results = pl.pallas_call(
+        functools.partial(gather_kernel, groups),
+        out_shape=[
+            jax.ShapeDtypeStruct((depth, block, size), values.dtype),
+            jax.ShapeDtypeStruct((depth, *gain.shape), gain.dtype),
+        ]
+        + [
+            jax.ShapeDtypeStruct((depth, 2 * 4, *shard.shape), shard.dtype) for shard in shards
+        ],
+        in_specs=[anywhere] * (2 + groups),
+        out_specs=[anywhere] * (2 + groups),
+        scratch_shapes=[
+            dma((depth,)),
+            dma((depth,)),
+            dma((depth,)),
+            dma((depth,)),
+            dma((groups,)),
+            dma((groups, depth)),
+            dma((groups, depth)),
+            dma((groups, depth, 3)),
+            dma((groups, depth, 4)),
+            dma((groups, depth, 4)),
+            dma((groups, depth, 4)),
+        ],
+        compiler_params=pltpu.CompilerParams(collective_id=1, has_side_effects=True),
+        name="gather_all",
+    )(values, gain, *shards)
+    return results[0], results[1], results[2:]
+
+
+def add_into(total, part):
+    rows = total.shape[0]
+    step = 32 if rows % 32 == 0 else 16
+
+    @pl.loop(0, rows // step)
+    def _(at):
+        here = pl.ds(pl.multiple_of(at * step, step), step)
+        total[here, :] = (
+            total[here, :].astype(jnp.float32) + part[here, :].astype(jnp.float32)
+        ).astype(total.dtype)
+
+
+def scatter_kernel(groups, values_ref, gain_ref, *refs):
+    parts, refs = refs[:groups], refs[groups:]
+    rows_ref, gain_out = refs[:2]
+    outs, refs = refs[2 : 2 + groups], refs[2 + groups :]
+    halves = refs[:groups]
+    passed = refs[groups : 2 * groups]
+    landed = refs[2 * groups : 3 * groups]
+    staged = refs[3 * groups : 4 * groups]
+    gain_sum, gain_in = refs[4 * groups : 4 * groups + 2]
+    (x_send, x_recv, g_send, g_recv, l_sem, c_send, c_recv, p_send, p_recv, z_send, z_recv) = refs[
+        4 * groups + 2 :
+    ]
+    pair, core, place = places()
+    depth = CLIPS_PER_COLUMN
+    greet(pair, core, place)
+
+    def remote(source, target, send, recv, where):
+        return pltpu.make_async_remote_copy(
+            src_ref=source,
+            dst_ref=target,
+            send_sem=send,
+            recv_sem=recv,
+            device_id=where,
+            device_id_type=MESH_ID,
+        )
+
+    sends = []
+
+    def send(source, target, send_sem, recv_sem, where):
+        copy = remote(source, target, send_sem, recv_sem, where)
+        copy.start()
+        sends.append(copy)
+
+    def arrived(target, sem):
+        remote(target, target, sem, sem, device(pair ^ 1, core, place)).wait_recv()
+
+    def block(group, step, other, flip):
+        return parts[group].at[place ^ step, 2 * (pair ^ other) + (core ^ flip)]
+
+    mine = (place % 2) * 2 + core
+    block_width = rows_ref.shape[0]
+    size = values_ref.shape[1]
+    moves = []
+    for step in range(depth):
+        to_core, to_place = place // 2, mine ^ step
+        source = values_ref.at[
+            pl.ds(pl.multiple_of(to_place * block_width, block_width), block_width), :
+        ]
+        target = rows_ref.at[:, pl.ds(pl.multiple_of(mine * size, size), size)]
+        copy = remote(
+            source, target, x_send.at[step], x_recv.at[step], device(pair, to_core, to_place)
+        )
+        local = pltpu.make_async_copy(source, target, x_recv.at[step])
+        away = (to_core != core) | (to_place != place)
+        moves.append((away, copy))
+
+        @pl.when(away)
+        def _():
+            copy.start()
+
+        @pl.when(jnp.logical_not(away))
+        def _():
+            local.start()
+
+    for step in range(1, depth):
+        send(
+            gain_ref.at[place ^ step],
+            gain_in.at[step],
+            g_send.at[step],
+            g_recv.at[step],
+            device(pair, core, place ^ step),
+        )
+
+    def gain_column():
+        total = gain_ref[place]
+        for step in range(1, depth):
+            arrived(gain_in.at[step], g_recv.at[step])
+            total += gain_in[step]
+        gain_sum[0] = total
+        gain_hop(0)
+
+    def gain_hop(at):
+        send(
+            gain_sum.at[at],
+            gain_in.at[depth + at],
+            g_send.at[depth + at],
+            g_recv.at[depth + at],
+            [
+                device(pair, core ^ 1, place),
+                device(pair ^ 1, core, place),
+                device(pair ^ 2, core, place),
+            ][at],
+        )
+
+    def gain_land(at):
+        arrived(gain_in.at[depth + at], g_recv.at[depth + at])
+        total = gain_sum[at] + gain_in[depth + at]
+        if at < 2:
+            gain_sum[at + 1] = total
+            gain_hop(at + 1)
+        else:
+            gain_out[...] = total
+
+    order = [(group, step) for step in (1, 2, 3, 0) for group in range(groups)]
+    for group, step in order:
+        for other in range(4):
+            send(
+                block(group, step, other, 1),
+                halves[group].at[step, other],
+                c_send.at[group, step, other],
+                c_recv.at[group, step, other],
+                device(pair, core ^ 1, place),
+            )
+
+    def load(at):
+        group, step = order[at]
+        copies = []
+        for other in range(4):
+            copy = pltpu.make_async_copy(
+                block(group, step, other, 0),
+                staged[group].at[step % 2, other],
+                l_sem.at[group, step % 2, other],
+            )
+            copy.start()
+            copies.append(copy)
+        return copies
+
+    def ways(group, step):
+        return (1, 2) if (group + step) % 2 == 0 else (2, 1)
+
+    def first_hop(group, step, loads):
+        near, far = ways(group, step)
+        for other in (near, 3, far, 0):
+            half = halves[group].at[step, other]
+            arrived(half, c_recv.at[group, step, other])
+            loads[other].wait()
+            add_into(half, staged[group].at[step % 2, other])
+            if other == near or other == 3:
+                slot = 0 if other == near else 1
+                send(
+                    half,
+                    passed[group].at[step, slot],
+                    p_send.at[group, step, slot],
+                    p_recv.at[group, step, slot],
+                    device(pair ^ near, core, place),
+                )
+
+    def second_hop(group, step):
+        near, far = ways(group, step)
+        arrived(passed[group].at[step, 1], p_recv.at[group, step, 1])
+        add_into(halves[group].at[step, far], passed[group].at[step, 1])
+        send(
+            halves[group].at[step, far],
+            passed[group].at[step, 2],
+            p_send.at[group, step, 2],
+            p_recv.at[group, step, 2],
+            device(pair ^ far, core, place),
+        )
+        arrived(passed[group].at[step, 0], p_recv.at[group, step, 0])
+        add_into(halves[group].at[step, 0], passed[group].at[step, 0])
+
+    def last_hop(group, step):
+        arrived(passed[group].at[step, 2], p_recv.at[group, step, 2])
+        add_into(halves[group].at[step, 0], passed[group].at[step, 2])
+        if step:
+            send(
+                halves[group].at[step, 0],
+                landed[group].at[step - 1],
+                z_send.at[group, step],
+                z_recv.at[group, step],
+                device(pair, core, place ^ step),
+            )
+
+    loads = {0: load(0)}
+    for at in range(len(order) + 4):
+        if at + 1 < len(order):
+            loads[at + 1] = load(at + 1)
+        if at < len(order):
+            first_hop(*order[at], loads[at])
+        if 0 <= at - 2 < len(order):
+            second_hop(*order[at - 2])
+        if 0 <= at - 4:
+            last_hop(*order[at - 4])
+        if at == 2:
+            gain_column()
+        if at in (4, 6, 8):
+            gain_land((at - 4) // 2)
+    for group in range(groups):
+        for step in range(1, depth):
+            arrived(landed[group].at[step - 1], z_recv.at[group, step])
+        rows = outs[group].shape[0]
+        unit = 32 if rows % 32 == 0 else 16
+
+        @pl.loop(0, rows // unit)
+        def _(at):
+            here = pl.ds(pl.multiple_of(at * unit, unit), unit)
+            total = halves[group][0, 0, here, :].astype(jnp.float32)
+            for step in range(1, depth):
+                total += landed[group][step - 1, here, :].astype(jnp.float32)
+            outs[group][here, :] = total
+
+    for copy in sends:
+        copy.wait_send()
+    for step in range(depth):
+        chunk = place ^ step
+        from_core, from_place = chunk % 2, 2 * core + chunk // 2
+        target = rows_ref.at[:, pl.ds(pl.multiple_of(chunk * size, size), size)]
+        foreign = (from_core != core) | (from_place != place)
+        away, copy = moves[step]
+
+        @pl.when(foreign)
+        def _():
+            arrived(target, x_recv.at[step])
+
+        @pl.when(jnp.logical_not(foreign))
+        def _():
+            pltpu.make_async_copy(target, target, x_recv.at[step]).wait()
+
+        @pl.when(away)
+        def _():
+            copy.wait_send()
+
+
+def scatter_all(values, gain, parts):
+    groups = len(parts)
+    depth = CLIPS_PER_COLUMN
+    width, size = values.shape
+    dma = pltpu.SemaphoreType.DMA
+    anywhere = pl.BlockSpec(memory_space=pl.ANY)
+    inside = pl.BlockSpec(memory_space=pltpu.VMEM)
+    shapes = [part.shape[2:] for part in parts]
+    low = jnp.bfloat16
+    results = pl.pallas_call(
+        functools.partial(scatter_kernel, groups),
+        out_shape=[
+            jax.ShapeDtypeStruct((width // depth, size * depth), values.dtype),
+            jax.ShapeDtypeStruct(gain.shape[1:], gain.dtype),
+        ]
+        + [jax.ShapeDtypeStruct(shape, jnp.float32) for shape in shapes],
+        in_specs=[anywhere, inside] + [anywhere] * groups,
+        out_specs=[anywhere, inside] + [inside] * groups,
+        scratch_shapes=[pltpu.VMEM((depth, 4, *shape), low) for shape in shapes]
+        + [pltpu.VMEM((depth, 3, *shape), low) for shape in shapes]
+        + [pltpu.VMEM((depth - 1, *shape), low) for shape in shapes]
+        + [pltpu.VMEM((2, 4, *shape), low) for shape in shapes]
+        + [
+            pltpu.VMEM((3, *gain.shape[1:]), gain.dtype),
+            pltpu.VMEM((depth + 3, *gain.shape[1:]), gain.dtype),
+            dma((depth,)),
+            dma((depth,)),
+            dma((depth + 3,)),
+            dma((depth + 3,)),
+            dma((groups, 2, 4)),
+            dma((groups, depth, 4)),
+            dma((groups, depth, 4)),
+            dma((groups, depth, 3)),
+            dma((groups, depth, 3)),
+            dma((groups, depth)),
+            dma((groups, depth)),
+        ],
+        cost_estimate=pl.CostEstimate(
+            flops=200_000_000_000, bytes_accessed=500_000_000, transcendentals=0
+        ),
+        compiler_params=pltpu.CompilerParams(
+            collective_id=2, has_side_effects=True, vmem_limit_bytes=60 << 20
+        ),
+        name="scatter_all",
+    )(values, gain, *parts)
+    return results[0], results[1], results[2:]
+
+
+def outer_kernel(former_ref, latter_ref, out_ref):
+    out_ref[0] = lax.dot_general(
+        former_ref[...],
+        latter_ref[0],
+        (((1,), (1,)), ((), ())),
+        preferred_element_type=jnp.float32,
+    ).astype(out_ref.dtype)
+
+
+def outer(former, latter):
+    width, size = former.shape
+    depth, columns, _ = latter.shape
+    tile = width // 2
+    return pl.pallas_call(
+        outer_kernel,
+        out_shape=jax.ShapeDtypeStruct((depth, width, columns), jnp.bfloat16),
+        grid=(depth, width // tile),
+        in_specs=[
+            pl.BlockSpec((tile, size), lambda at, row: (row, 0)),
+            pl.BlockSpec((1, columns, size), lambda at, row: (at, 0, 0)),
+        ],
+        out_specs=pl.BlockSpec((1, tile, columns), lambda at, row: (at, row, 0)),
+        cost_estimate=pl.CostEstimate(
+            flops=2 * depth * width * columns * size,
+            bytes_accessed=2 * depth * width * columns,
+            transcendentals=0,
+        ),
+        name="outer",
+    )(former, latter)
+
+
+def gather_every(values, gains, shards, depth):
+    count, block = gains.shape
+    if paved():
+        padded = jnp.pad(gains, ((0, 8 - count), (0, 0)))
+        tokens, gains, wholes = gather_all(values, padded, shards)
+        tokens = tokens.reshape(-1, tokens.shape[2])
+    else:
+        tokens = to_tokens(values, depth)
+        gains = lax.all_gather(gains, COL, axis=0)
+        wholes = [lax.all_gather(shard, EVERY, axis=0, tiled=True) for shard in shards]
+    gains = gains[:, :count].transpose(1, 0, 2).reshape(count, depth * block)
+    return (
+        tokens,
+        gains,
+        [whole.reshape(depth, -1, shard.shape[1]) for whole, shard in zip(wholes, shards)],
+    )
+
+
+def scatter_every(values, gains, parts, rows, depth):
+    count, width = gains.shape
+    if paved():
+        blocks = gains.reshape(count, depth, width // depth).transpose(1, 0, 2)
+        values, gains, sums = scatter_all(
+            values,
+            jnp.pad(blocks, ((0, 0), (0, 8 - count), (0, 0))),
+            [part.reshape(part.shape[0], -1, rows, part.shape[2]) for part in parts],
+        )
+        return values, gains[:count], sums
+    gains = lax.dynamic_slice_in_dim(
+        lax.psum(gains, EVERY), lax.axis_index(COL) * (width // depth), width // depth, 1
+    )
+    return (
+        to_features(values, depth),
+        gains,
+        [
+            lax.psum_scatter(
+                part.reshape(-1, part.shape[2]), EVERY, scatter_dimension=0, tiled=True
+            ).astype(jnp.float32)
+            for part in parts
+        ],
+    )
+
+
+def paved():
+    return lax.axis_size("pair") == 4 and lax.axis_size(COL) == CLIPS_PER_COLUMN
+
+
 def attend_kernel(team, valid_ref, *refs):
-    query_ref, keys, values = refs[0], refs[1 : 1 + team], refs[1 + team : 1 + 2 * team]
-    out_ref, log_ref, wide_keys, wide_values = refs[1 + 2 * team :]
+    own_ref, others = refs[0], refs[1:team]
+    query_ref = own_ref.at[0, 2, 0]
+    keys = [ref.at[0, 0, 0] for ref in (own_ref, *others)]
+    values = [ref.at[0, 1, 0] for ref in (own_ref, *others)]
+    out_ref, log_ref, wide_keys, wide_values = refs[team:]
     dim, size = query_ref.shape
     scale = math.log2(math.e) / math.sqrt(HEAD_DIM)
     pad = (SPARE, size)
@@ -136,12 +736,16 @@
 
 
 def attend_back_kernel(team, valid_ref, *refs):
-    query_ref, out_ref, grad_ref, log_ref = refs[:4]
-    keys, values = refs[4 : 4 + team], refs[4 + team : 4 + 2 * team]
-    query_grad_ref = refs[4 + 2 * team]
-    key_grads = refs[5 + 2 * team : 5 + 3 * team]
-    value_grads = refs[5 + 3 * team : 5 + 4 * team]
-    wide_keys, wide_values, flat_keys, key_total, value_total = refs[5 + 4 * team :]
+    out_ref, grad_ref, log_ref, own_ref = refs[:4]
+    others = refs[4 : 3 + team]
+    query_ref = own_ref.at[0, 2, 0]
+    keys = [ref.at[0, 0, 0] for ref in (own_ref, *others)]
+    values = [ref.at[0, 1, 0] for ref in (own_ref, *others)]
+    grads = refs[3 + team : 3 + 2 * team]
+    query_grad_ref = grads[0].at[0, 2, 0]
+    key_grads = [ref.at[0, 0, 0] for ref in grads]
+    value_grads = [ref.at[0, 1, 0] for ref in grads]
+    wide_keys, wide_values, flat_keys, key_total, value_total = refs[3 + 2 * team :]
     dim, size = query_ref.shape
     base = 1.0 / math.sqrt(HEAD_DIM)
     scale = math.log2(math.e) * base
@@ -197,14 +801,18 @@
         value_grads[at][...] = value_total[part, :].T.astype(jnp.bfloat16)
 
 
-def head_specs(size, count):
-    return [pl.BlockSpec((HEAD_DIM, size), lambda head, *_: (head, 0)) for _ in range(count)]
-
-
-def attend(query, keys, values, valid):
-    width, size = query.shape
-    team = len(keys)
-    heads = width // HEAD_DIM
+def part_spec(parts, per_block, size):
+    return pl.BlockSpec(
+        (1, parts, 1, HEAD_DIM, size),
+        lambda head, *_: (head // per_block, 0, head % per_block, 0, 0),
+    )
+
+
+def attend(own, others, valid):
+    depth, _, per_block, _, size = own.shape
+    heads = depth * per_block
+    width = heads * HEAD_DIM
+    team = 1 + len(others)
     span = team * size
     row_spec = pl.BlockSpec((1, 1, size), lambda head, *_: (head, 0, 0))
     return pl.pallas_call(
@@ -216,37 +824,40 @@
         grid_spec=pltpu.PrefetchScalarGridSpec(
             num_scalar_prefetch=1,
             grid=(heads,),
-            in_specs=head_specs(size, 1 + 2 * team),
-            out_specs=(head_specs(size, 1)[0], row_spec),
+            in_specs=[part_spec(3, per_block, size)]
+            + [part_spec(2, per_block, size) for _ in others],
+            out_specs=(pl.BlockSpec((HEAD_DIM, size), lambda head, *_: (head, 0)), row_spec),
             scratch_shapes=[
                 pltpu.VMEM((span, 2 * HEAD_DIM + SPARE), jnp.bfloat16),
                 pltpu.VMEM((HEAD_DIM + SPARE, span), jnp.bfloat16),
             ],
         ),
         cost_estimate=pl.CostEstimate(
-            flops=4 * width * size * span,
+            flops=12 * width * size * span,
             bytes_accessed=2 * width * size * (2 + 2 * team),
             transcendentals=heads * size * span,
         ),
         name="attend",
-    )(valid, query, *keys, *values)
-
-
-def attend_back(query, out, grad, logs, keys, values, valid):
-    width, size = query.shape
-    team = len(keys)
-    heads = width // HEAD_DIM
+    )(valid, own, *others)
+
+
+def attend_back(own, others, out, grad, logs, valid):
+    depth, _, per_block, _, size = own.shape
+    heads = depth * per_block
+    width = heads * HEAD_DIM
+    team = 1 + len(others)
     span = team * size
     row_spec = pl.BlockSpec((1, 1, size), lambda head, *_: (head, 0, 0))
-    shape = jax.ShapeDtypeStruct((width, size), jnp.bfloat16)
+    head_spec = pl.BlockSpec((HEAD_DIM, size), lambda head, *_: (head, 0))
+    part_specs = [part_spec(3, per_block, size)] + [part_spec(2, per_block, size) for _ in others]
     results = pl.pallas_call(
         functools.partial(attend_back_kernel, team),
-        out_shape=(shape,) * (1 + 2 * team),
+        out_shape=[jax.ShapeDtypeStruct(array.shape, jnp.bfloat16) for array in (own, *others)],
         grid_spec=pltpu.PrefetchScalarGridSpec(
             num_scalar_prefetch=1,
             grid=(heads,),
-            in_specs=head_specs(size, 3) + [row_spec] + head_specs(size, 2 * team),
-            out_specs=head_specs(size, 1 + 2 * team),
+            in_specs=[head_spec, head_spec, row_spec] + part_specs,
+            out_specs=part_specs,
             scratch_shapes=[
                 pltpu.VMEM((span, 2 * HEAD_DIM + SPARE), jnp.bfloat16),
                 pltpu.VMEM((span, HEAD_DIM + SPARE), jnp.bfloat16),
@@ -256,13 +867,13 @@
             ],
         ),
         cost_estimate=pl.CostEstimate(
-            flops=10 * width * size * span,
+            flops=30 * width * size * span,
             bytes_accessed=2 * width * size * (4 + 4 * team),
             transcendentals=heads * size * span,
         ),
         name="attend_back",
-    )(valid, query, out, grad, logs, *keys, *values)
-    return results[0], results[1 : 1 + team], results[1 + team :]
+    )(valid, out, grad, logs, own, *others)
+    return results[0], results[1:]
 
 
 def normalize(values):
@@ -294,18 +905,6 @@
     weight_next = weight - rate * (gradient + MOMENTUM * moment_next)
     average_next = AVERAGING * average + (1.0 - AVERAGING) * weight_next
     return (moment_next, weight_next, average_next)
-
-
-def gather_weight(shard, depth):
-    whole = lax.all_gather(shard, EVERY, axis=0, tiled=True)
-    return whole.reshape(depth, whole.shape[0] // depth, shard.shape[1])
-
-
-def scatter_grad(parts):
-    depth, width, columns = parts.shape
-    return lax.psum_scatter(
-        parts.reshape(depth * width, columns), EVERY, scatter_dimension=0, tiled=True
-    ).astype(jnp.float32)
 
 
 def on_device(
@@ -337,44 +936,48 @@
     rows_of_weight = project_weight.shape[1]
     width = block_width * depth
     size = rows_local // depth
+    per_block = block_width // HEAD_DIM
     bf16 = jnp.bfloat16
-
-    project_full = gather_weight(
-        project_weight.astype(bf16).transpose(1, 0, 2).reshape(rows_of_weight, 3 * block_width),
+    core = lax.axis_index("core")
+
+    shard = project_weight.astype(bf16)
+    resident, gains, (project_full, output_full, expand_full, reduce_full) = gather_every(
+        inputs,
+        jnp.stack([gain_first, gain_second]),
+        [
+            jnp.concatenate([shard[1], shard[2], shard[0]], axis=1),
+            output_weight.astype(bf16).T,
+            expand_weight.astype(bf16),
+            reduce_weight.astype(bf16).T,
+        ],
         depth,
     )
-    output_full = gather_weight(output_weight.astype(bf16).T, depth)
-    expand_full = gather_weight(expand_weight.astype(bf16), depth)
-    reduce_full = gather_weight(reduce_weight.astype(bf16).T, depth)
-    gains = lax.all_gather(jnp.stack([gain_first, gain_second]), COL, axis=1, tiled=True)
-    lengths = lax.all_gather(clip_lengths, "core", axis=0, tiled=True)
-
-    clip = lax.axis_index("zhi")
-    length = lax.dynamic_index_in_dim(lengths, clip, 0, False)
+    resident = resident.astype(jnp.float32)
+
+    other_lengths = exchange(clip_lengths, "core", 1, 2)
+    lengths = jnp.where(
+        core == 0,
+        jnp.concatenate([clip_lengths, other_lengths]),
+        jnp.concatenate([other_lengths, clip_lengths]),
+    )
+    length = lax.dynamic_index_in_dim(lengths, lax.axis_index("zhi"), 0, False)
     slot = lax.axis_index(TEAM)
     valid = jnp.clip(
         jnp.stack([length - (slot ^ step) * size for step in range(team)]), 0, size
     ).astype(jnp.int32)
     token_mask = (jnp.arange(size, dtype=jnp.int32) < valid[0]).astype(jnp.float32)[None, :]
 
-    resident = to_tokens(inputs, depth).astype(jnp.float32)
     normed_one, inverse_one = normalize(resident)
     hidden_one = (normed_one * gains[0][:, None]).astype(bf16)
-    projected = product(
-        "zdke,dt->kzet",
-        project_full.reshape(depth, width, 3, block_width),
-        hidden_one,
-        bf16,
-    ).reshape(3, width, size)
-    query = projected[0]
-    both = projected[1:]
-    others = [exchange(both, TEAM, step, team) for step in range(1, team)]
-    keys = [both[0]] + [other[0] for other in others]
-    values = [both[1]] + [other[1] for other in others]
-    attended, logs = attend(query, keys, values, valid)
-    middle = resident + product(
-        "zde,zet->dt", output_full, attended.reshape(depth, block_width, size)
-    )
+    own = product("zdu,dt->zut", project_full, hidden_one, bf16).reshape(
+        depth, 3, per_block, HEAD_DIM, size
+    )
+    others = [exchange(own[:, :2], TEAM, step, team) for step in range(1, team)]
+    cotangent, *others = lax.optimization_barrier((cotangent, *others))
+    upstream_low = to_tokens(cotangent, depth) * token_mask.astype(bf16)
+    attended, logs = attend(own, others, valid)
+    attended_blocks = attended.reshape(depth, block_width, size)
+    middle = resident + product("zde,zet->dt", output_full, attended_blocks)
     normed_two, inverse_two = normalize(middle)
     hidden_two = (normed_two * gains[1][:, None]).astype(bf16)
     pre_act = product("zdu,dt->zut", expand_full, hidden_two)
@@ -384,47 +987,45 @@
         (middle + product("zdu,zut->dt", reduce_full, activated)).astype(bf16), depth
     )
 
-    upstream_low = to_tokens(cotangent, depth) * token_mask.astype(bf16)
     upstream = upstream_low.astype(jnp.float32)
-    reduce_grad = scatter_grad(product("dt,zut->zdu", upstream_low, activated, bf16)).T
+    reduce_part = product("dt,zut->zdu", upstream_low, activated, bf16)
     pre_grad = (
         product("zdu,dt->zut", reduce_full, upstream_low) * slope.astype(jnp.float32)
     ).astype(bf16)
-    expand_grad = scatter_grad(product("dt,zut->zdu", hidden_two, pre_grad, bf16))
+    expand_part = product("dt,zut->zdu", hidden_two, pre_grad, bf16)
     normed_two_grad = product("zdu,zut->dt", expand_full, pre_grad)
     middle_grad, gain_two_part = normalize_back(normed_two_grad, normed_two, inverse_two, gains[1])
     middle_grad = middle_grad + upstream
     middle_grad_low = middle_grad.astype(bf16)
-    output_grad = scatter_grad(
-        product(
-            "dt,zet->zde", middle_grad_low, attended.reshape(depth, block_width, size), bf16
-        )
-    ).T
+    output_part = outer(middle_grad_low, attended_blocks)
     attended_grad = product("zde,dt->zet", output_full, middle_grad_low, bf16).reshape(width, size)
-    query_grad, key_grads, value_grads = attend_back(
-        query, attended, attended_grad, logs, keys, values, valid
-    )
-    pair_grad = jnp.stack([key_grads[0], value_grads[0]]).astype(jnp.float32)
+    own_grad, other_grads = attend_back(own, others, attended, attended_grad, logs, valid)
+    own_grad, block_output = lax.optimization_barrier((own_grad, block_output))
+    pair_grad = own_grad[:, :2].astype(jnp.float32)
     for step in range(1, team):
-        pair_grad = pair_grad + exchange(
-            jnp.stack([key_grads[step], value_grads[step]]), TEAM, step, team
-        ).astype(jnp.float32)
-    stacked = jnp.concatenate([query_grad[None], pair_grad.astype(bf16)]).reshape(
-        3, depth, block_width, size
-    )
-    project_grad = scatter_grad(
-        product("dt,kzet->zdke", hidden_one, stacked, bf16).reshape(depth, width, 3 * block_width)
-    )
-    project_grad = project_grad.reshape(rows_of_weight, 3, block_width).transpose(1, 0, 2)
-    normed_one_grad = product(
-        "zdke,kzet->dt", project_full.reshape(depth, width, 3, block_width), stacked
-    )
+        pair_grad = pair_grad + exchange(other_grads[step - 1], TEAM, step, team).astype(
+            jnp.float32
+        )
+    stacked = jnp.concatenate([pair_grad.astype(bf16), own_grad[:, 2:]], axis=1).reshape(
+        depth, 3 * block_width, size
+    )
+    project_part = outer(hidden_one, stacked)
+    normed_one_grad = product("zdu,zut->dt", project_full, stacked)
     input_grad, gain_one_part = normalize_back(normed_one_grad, normed_one, inverse_one, gains[0])
-    input_grad = to_features((input_grad + middle_grad).astype(bf16), depth).astype(jnp.float32)
-    gain_grads = lax.psum_scatter(
-        lax.psum(jnp.stack([gain_one_part, gain_two_part]), ROW), COL, scatter_dimension=1, tiled=True
-    )
+    input_grad, gain_grads, weight_grads = scatter_every(
+        (input_grad + middle_grad).astype(bf16),
+        jnp.stack([gain_one_part, gain_two_part]),
+        [reduce_part, expand_part, project_part, output_part],
+        rows_of_weight,
+        depth,
+    )
+    input_grad = input_grad.astype(jnp.float32)
     gain_one_grad, gain_two_grad = gain_grads[0], gain_grads[1]
+    reduce_grad, expand_grad, project_grad, output_grad = weight_grads
+    reduce_grad, output_grad = reduce_grad.T, output_grad.T
+    project_grad = jnp.stack(
+        [project_grad[:, at * block_width : (at + 1) * block_width] for at in (2, 0, 1)]
+    )
 
     scale = 1.0 / math.sqrt(rows_local * lax.axis_size(ROW))
     pm, pw, pa = update(

time: 1230 us -> 807 us (0.66)
  waiting for transfers between devices: 548 us -> 5.89 us
  Pallas kernels: 109 us -> 545 us
  local copies, waits for them, and re-layouts: 173 us -> 26.8 us
  blocking collectives: 115 us -> 0 us
  matrix products: 166 us -> 143 us
  between operations: 17 us -> 3.1 us
    pallas_call x1 -> x5, Pallas kernels: 60.4 us -> 496 us  [the longest x1 207 us: scatter_all(): pl.pallas_call(functools.partial(scatter_kernel, groups), out_shape=[jax....]
    reduce_scatter x3 -> x0, waiting for transfers between devices: 339 us -> none  [scatter_grad(): lax.psum_scatter(parts.reshape(depth * width, columns), EVERY, scatter_di...]
    all_gather x4 -> x0, waiting for transfers between devices: 106 us -> none  [gather_weight(): whole = lax.all_gather(shard, EVERY, axis=0, tiled=True)]
    all_gather x1 -> x0, blocking collectives: 97.5 us -> none  [on_device(): lax.all_gather(jnp.stack([gain_first, gain_second]), COL, axis=1, tiled=T...]
    ppermute x8 -> x4, waiting for transfers between devices: 76.1 us -> 0.01 us  [to_features(): piece = lax.ppermute(chunk, COLUMN, back)]
    unnamed x104 -> x110, local copies, waits for them, and re-layouts: 75.3 us -> 5.44 us
    dot_general x12 -> x10, matrix products: 166 us -> 143 us  [product(): jnp.einsum(spec, former, latter, preferred_element_type=jnp.float32)]
    ppermute x8 -> x4, waiting for transfers between devices: 19.4 us -> 0.01 us  [to_tokens(): pieces.append(lax.ppermute(chunk, COLUMN, column_pairs(depth, step)))]
  transfers between devices with their start and end apart: 27 -> 11, of which waited for: 11 -> 1; matrix products, arithmetic and copies ran while one was open for 22% -> 17% of each run, Pallas kernels for 4% -> 9%
where the time goes in v2:
time: 807 us; the launch traced here: 798 us
  Pallas kernels  545 us (68%)
  matrix products  143 us (18%)
  other arithmetic  41.4 us (5%)
  starting transfers between devices  32 us (4%)
  local copies, waits for them, and re-layouts  26.8 us (3%)
    pallas_call x1, Pallas kernels, scatter_all(): pl.pallas_call(functools.partial(scatter_kernel, groups), out_shape=[jax....  207 us
    pallas_call x1, Pallas kernels, gather_all(): pl.pallas_call(functools.partial(gather_kernel, groups), out_shape=[jax.S...  202 us
    dot_general x10, matrix products, product(): jnp.einsum(spec, former, latter, preferred_element_type=jnp.float32)  143 us
    pallas_call x1, Pallas kernels, attend_back(): pl.pallas_call(functools.partial(attend_back_kernel, team), out_shape=[ja...  61.1 us
    pallas_call x1, Pallas kernels, attend(): pl.pallas_call(functools.partial(attend_kernel, team), out_shape=(jax.Sha...  49.2 us
    pallas_call x2, Pallas kernels, outer(): pl.pallas_call(outer_kernel, out_shape=jax.ShapeDtypeStruct((depth, width...  25.5 us
    ppermute x4, starting transfers between devices, to_tokens(): pieces.append(lax.ppermute(chunk, COLUMN, column_pairs(depth, step)))  21 us
  transfers between devices with their start and end apart: 11, of which 1 were waited for; matrix products, arithmetic and copies ran while one was open for 17% of the time, Pallas kernels for 9%

profile of v2, /device:TPU:8, one launch (start us, length us, event | category | flops | bytes accessed | tf_op | source)
XLA Modules:
  0.0 797.5 jit_solution(3969856898554911764)
XLA Ops:
  4.9 1.9 convert_element_type.120.refs_2_
  9.1 202.1 %gather_all.1 = (bf16[4,320,768]{2,1,0:T(8,128)(2,1)}, f32[4,8,320]{2,1,0:T(8,128)}, bf16[4,8,160,960]{3,2,1,0:T(8,128)(2,1)}, bf16[4,8,160,320]{3,2,1,0:T(8,128...) custom-call(bf16[320,3072]{1,0:T(8,128)(2,1)} %values_ref.1, ...), custom_call_target="tpu_custom_call" | custom-call | tf_op jit(solution)/shard_map/gather_all/pallas_call | solution.py:295
  212.1 2.1 convert_reduce_fusion
  214.2 2.2 fusion.10
  216.4 10.8 %convolution_convert_fusion.2 = bf16[4,960,768]{2,1,0:T(8,128)(2,1)S(1)} fusion(bf16[4,1280,960]{2,1,0:T(8,128)(2,1)} %bitcast.168, bf16[1280,768,1]{1,0,2:T(8,128)(2,1)S(1)} %bitcast.156), kind=kOutput, calls=%fused_computation.47 | convolution fusion | flops 7552696320 | bytes 17694720 | tf_op jit(solution)/shard_map/zdu,dt->zut/dot_general | solution.py:900
  227.2 2.4 slice.71
  232.2 5.9 collective-permute-done
  240.6 49.2 %attend.1 = (bf16[1280,768]{1,0:T(8,128)(2,1)}, f32[16,1,768]{2,1,0:T(1,128)}) custom-call(s32[2]{0:T(128)} %copy-done.45, bf16[4,3,4,80,768]{4,3,2,1,0:T(8,128)(2,1)} %bitcast.154, bf16[4,2,4,80,768]{4,3,2,1,0:T(8,128)(2,1)} %collective-permute-done.1.refs_1_.refs_4_), custom_call_target="tpu_custom_call" | custom-call | flops 18119393280 | bytes 11796480 | tf_op jit(solution)/shard_map/attend/pallas_call | solution.py:818
  290.8 16.0 %collective-permute-start.4 = (bf16[320,768]{1,0:T(8,128)(2,1)S(1)}, bf16[320,768]{1,0:T(8,128)(2,1)S(1)}, u32[]{:S(2)}, u32[]{:S(2)}) collective-permute-start(bf16[320,768]{1,0:T(8,128)(2,1)S(1)} %get-tuple-element.116), channel_id=1, source_target_pairs={{0,1},{1,5},{2,0},{3,4},{4,3},{5,7},{6,2},{7,6},{8,9},{9,13},{10,8... | collective-permute-start | bytes 1474568 | tf_op jit(solution)/shard_map/ppermute | solution.py:69
  306.8 4.2 collective-permute-start.2
  311.0 5.1 multiply_reduce_fusion.1
  316.2 18.2 %multiply_convert_fusion = (bf16[4,1280,768]{2,1,0:T(8,128)(2,1)S(1)}, f32[4,1280,768]{2,1,0:T(8,128)}) fusion(bf16[4,1280,1280]{2,1,0:T(8,128)(2,1)} %bitcast.164, f32[1280,768]{1,0:T(8,128)S(1)} %get-tuple-element.129, f32[1280]{0:T(1024)S(1)} %mul.348, f32[768]{0:T(1024)S(1)} %get-tuple-element.126, f32[768]{0:T(1024)S(1)} %get-tuple-element.125), kind=kOutput, calls=%fused_computation.8 | convolution fusion | flops 10089922560 | bytes 40643584 | tf_op jit(solution)/shard_map/zdu,dt->zut/dot_general | solution.py:900
  334.4 15.9 %fusion.6 = bf16[1280,768]{1,0:T(8,128)(2,1)S(1)} fusion(f32[1280,768]{1,0:T(8,128)S(1)} %get-tuple-element.129, bf16[4,1280,1280]{2,1,0:T(8,128)(2,1)} %bitcast.166, bf16[4,1280,768]{2,1,0:T(8,128)(2,1)S(1)} %get-tuple-element.131), kind=kOutput, calls=%fused_computation.17 | convolution fusion | flops 10068295680 | bytes 26869760 | tf_op jit(solution)/shard_map/zdu,zut->dt/dot_general | solution.py:900
  351.6 1.9 collective-permute-start.6
  353.5 2.8 collective-permute-start.7
  356.4 5.7 collective-permute-start.9
  362.4 22.9 %multiply_convert_fusion.1 = bf16[4,1280,768]{2,1,0:T(8,128)(2,1)S(1)} fusion(bf16[4,1280,1280]{2,1,0:T(8,128)(2,1)} %bitcast.167, f32[4,1280,768]{2,1,0:T(8,128)} %get-tuple-element.132, bf16[320,768]{1,0:T(8,128)(2,1)S(1)} %get-tuple-element.111, bf16[320,768]{1,0:T(8,128)(2,1)S(1)} %get-tuple-element.112, bf16[320,768]{1,0:T(8,128)(2,1)S(1)} %get-tuple-element.113, ...), kind=kOutput, calls=%fused_computation.9 | convolution fusion | flops 10123345920 | bytes 38667776 | tf_op jit(solution)/shard_map/zdu,dt->zut/dot_general | solution.py:900
  385.3 16.8 %fusion.7 = (f32[1280]{0:T(1024)S(1)}, f32[768]{0:T(1024)S(1)}, f32[768]{0:T(1024)S(1)}, f32[1280,768,1]{1,0,2:T(8,128)S(1)}) fusion(f32[1280,768]{1,0:T(8,128)S(1)} %get-tuple-element.129, f32[768]{0:T(1024)S(1)} %get-tuple-element.126, f32[768]{0:T(1024)S(1)} %get-tuple-element.125, f32[1280]{0:T(1024)S(1)} %mul.348, ...), kind=kOutput, calls=%fused_computation.20 | convolution fusion | flops 10074190848 | bytes 28858368 | tf_op jit(solution)/shard_map/zdu,zut->dt/dot_general | solution.py:900
  402.2 6.4 fusion.39
  408.6 4.1 fusion.29
  412.7 61.1 %attend_back.1 = (bf16[4,3,4,80,768]{4,3,2,1,0:T(8,128)(2,1)}, bf16[4,2,4,80,768]{4,3,2,1,0:T(8,128)(2,1)}) custom-call(s32[2]{0:T(128)} %copy-done.45, bf16[1280,768]{1,0:T(8,128)(2,1)} %get-tuple-element.54.refs_0_, bf16[1280,768]{1,0:T(8,128)(2,1)} %bitcast.178, f32[16,1,768]{2,1,0:T(1,128)} %get-tuple-element.59.refs_2_, ...), custom_call_target="tpu_custom_call" | custom-call | flops 45298483200 | bytes 23592960 | tf_op jit(solution)/shard_map/attend_back/pallas_call | solution.py:853
  477.2 1.8 constant_dynamic-update-slice_fusion.2
  482.7 3.0 slice.61
  485.7 10.2 %outer.3 = bf16[4,1280,320]{2,1,0:T(8,128)(2,1)} custom-call(bf16[1280,768]{1,0:T(8,128)(2,1)} %copy-done.17, bf16[4,320,768]{2,1,0:T(8,128)(2,1)} %bitcast.176), custom_call_target="tpu_custom_call" | custom-call | flops 2516582400 | bytes 3276800 | tf_op jit(solution)/shard_map/outer/pallas_call | solution.py:621
  495.9 18.9 %convolution_convert_fusion.1 = bf16[4,1280,1280]{1,2,0:T(8,128)(2,1)} fusion(bf16[4,1280,768]{2,1,0:T(8,128)(2,1)} %copy-done.50, bf16[320,768]{1,0:T(8,128)(2,1)S(1)} %get-tuple-element.111, bf16[320,768]{1,0:T(8,128)(2,1)S(1)} %get-tuple-element.112, bf16[320,768]{1,0:T(8,128)(2,1)S(1)} %copy-done.19, bf16[320,768]{1,0:T(8,128)(2,1)S(1)} %get-tuple-element.110, ...), kind=kOutput, calls=%fused_computation.1 | convolution fusion | flops 10082713600 | bytes 22939136 | tf_op jit(solution)/shard_map/dt,zut->zdu/dot_general | solution.py:900
  514.8 16.7 %convolution_convert_fusion = bf16[4,1280,1280]{1,2,0:T(8,128)(2,1)} fusion(bf16[4,1280,768]{2,1,0:T(8,128)(2,1)} %copy-done.49, f32[1280,768]{1,0:T(8,128)S(1)} %copy-done.5, f32[1280]{0:T(1024)S(1)} %mul.348, f32[768]{0:T(1024)S(1)} %get-tuple-element.126, f32[768]{0:T(1024)S(1)} %get-tuple-element.125), kind=kOutput, calls=%fused_computation | convolution fusion | flops 10076815360 | bytes 24914944 | tf_op jit(solution)/shard_map/dt,zut->zdu/dot_general | solution.py:900
  531.5 3.2 add_convert_fusion
  536.4 14.0 %fusion.5 = (f32[1280]{0:T(1024)S(1)}, f32[768]{0:T(1024)S(1)}, f32[768]{0:T(1024)S(1)}, bf16[1280,768]{1,0:T(8,128)(2,1)}, f32[1280,768,1]{1,0,2:T(8,128)}) fusion(bf16[4,320,768]{2,1,0:T(8,128)(2,1)S(1)} %copy-done.1, f32[768]{0:T(1024)S(1)} %copy-done.33, f32[768]{0:T(1024)S(1)} %copy-done.35, f32[1280]{0:T(1024)S(1)} %copy-done.36, ...), kind=kOutput, calls=%fused_computation.15 | convolution fusion | flops 7560557568 | bytes 23615488 | tf_op jit(solution)/shard_map/zdu,zut->dt/dot_general | solution.py:900
  550.5 15.3 %outer.2 = bf16[4,1280,960]{2,1,0:T(8,128)(2,1)} custom-call(bf16[1280,768]{1,0:T(8,128)(2,1)} %get-tuple-element.105.former_ref, bf16[4,960,768]{2,1,0:T(8,128)(2,1)} %bitcast.151), custom_call_target="tpu_custom_call" | custom-call | flops 7549747200 | bytes 9830400 | tf_op jit(solution)/shard_map/outer/pallas_call | solution.py:621
  566.4 5.9 fusion.20.values_ref
  572.3 207.2 %scatter_all.1 = (bf16[320,3072]{1,0:T(8,128)(2,1)}, f32[8,320]{1,0:T(8,128)}, f32[160,1280]{1,0:T(8,128)}, f32[160,1280]{1,0:T(8,128)}, f32[160,960]{1,0:T(8,128)}, /*index=5*/f32[160,320]{1,0:T(8,128)}) custom-call(bf16[1280,768]{1,0:T(8,128)(2,1)} %fusion.20.values_ref, f32[4,8,320]{2,1,0:T(8,128)} %pad.9.gain_ref, bf16[4,8,160,1280]{3,2,1,0:T(8,128)(2,1)} %bitcast.172, ...), custom_call_target="tpu_custom_call" | custom-call | flops 199999995904 | bytes 500000000 | tf_op jit(solution)/shard_map/scatter_all/pallas_call | solution.py:569
  779.6 4.1 convert_element_type.148
  (173 shorter events, 36.6 us)
Async XLA Ops:
  0.7 6.2 copy-start.7
  230.9 9.2 %collective-permute-start.1 = (bf16[4,2,4,80,768]{4,3,2,1,0:T(8,128)(2,1)}, bf16[4,2,4,80,768]{4,3,2,1,0:T(8,128)(2,1)}, u32[]{:S(2)}, u32[]{:S(2)}) collective-permute-start(bf16[4,2,4,80,768]{4,3,2,1,0:T(8,128)(2,1)} %slice.71), channel_id=1, source_target_pairs={{0,4},{4,0},{1,5},{5,1},{2,6},{6,2},{3,7},{7,3},{8,12},{12,8},{9,1... | collective-permute-start | bytes 11796488 | tf_op jit(solution)/shard_map/ppermute | solution.py:35
  230.9 7.1 collective-permute-start
  240.1 49.6 %copy-start.16 = (bf16[320,3072]{1,0:T(8,128)(2,1)S(1)}, bf16[320,3072]{1,0:T(8,128)(2,1)}, u32[]{:S(2)}) copy-start(bf16[320,3072]{1,0:T(8,128)(2,1)} %param.22) | copy-start | bytes 5898244
  289.7 21.3 %copy-start = (bf16[4,320,768]{2,1,0:T(8,128)(2,1)S(1)}, bf16[4,320,768]{2,1,0:T(8,128)(2,1)}, u32[]{:S(2)}) copy-start(bf16[4,320,768]{2,1,0:T(8,128)(2,1)} %get-tuple-element.51) | copy-start | bytes 5898244
  289.7 21.3 %copy-start.48 = (bf16[1280,768]{1,0:T(8,128)(2,1)S(1)}, bf16[1280,768]{1,0:T(8,128)(2,1)}, u32[]{:S(2)}) copy-start(bf16[1280,768]{1,0:T(8,128)(2,1)} %get-tuple-element.54.refs_0_) | copy-start | bytes 5898244
  290.0 63.5 %collective-permute-start.5 = (bf16[320,768]{1,0:T(8,128)(2,1)S(1)}, bf16[320,768]{1,0:T(8,128)(2,1)S(1)}, u32[]{:S(2)}, u32[]{:S(2)}) collective-permute-start(bf16[320,768]{1,0:T(8,128)(2,1)S(1)} %get-tuple-element.115), channel_id=1, source_target_pairs={{0,5},{1,1},{2,4},{3,0},{4,7},{5,3},{6,6},{7,2},{8,13},{9,9},{10,1... | collective-permute-start | bytes 1474568 | tf_op jit(solution)/shard_map/ppermute | solution.py:69
  290.8 65.5 %collective-permute-start.4 = (bf16[320,768]{1,0:T(8,128)(2,1)S(1)}, bf16[320,768]{1,0:T(8,128)(2,1)S(1)}, u32[]{:S(2)}, u32[]{:S(2)}) collective-permute-start(bf16[320,768]{1,0:T(8,128)(2,1)S(1)} %get-tuple-element.116), channel_id=1, source_target_pairs={{0,1},{1,5},{2,0},{3,4},{4,3},{5,7},{6,2},{7,6},{8,9},{9,13},{10,8... | collective-permute-start | bytes 1474568 | tf_op jit(solution)/shard_map/ppermute | solution.py:69
  306.8 49.6 %collective-permute-start.3 = (bf16[320,768]{1,0:T(8,128)(2,1)S(1)}, bf16[320,768]{1,0:T(8,128)(2,1)S(1)}, u32[]{:S(2)}, u32[]{:S(2)}) collective-permute-start(bf16[320,768]{1,0:T(8,128)(2,1)S(1)} %get-tuple-element.117), channel_id=1, source_target_pairs={{0,4},{1,0},{2,5},{3,1},{4,6},{5,2},{6,7},{7,3},{8,12},{9,8},{10,1... | collective-permute-start | bytes 1474568 | tf_op jit(solution)/shard_map/ppermute | solution.py:69
  306.8 55.2 %collective-permute-start.2 = (bf16[320,768]{1,0:T(8,128)(2,1)S(1)}, bf16[320,768]{1,0:T(8,128)(2,1)S(1)}, u32[]{:S(2)}, u32[]{:S(2)}) collective-permute-start(bf16[320,768]{1,0:T(8,128)(2,1)S(1)} %get-tuple-element.114), channel_id=1, source_target_pairs={{0,0},{1,4},{2,1},{3,5},{4,2},{5,6},{6,3},{7,7},{8,8},{9,12},{10,9... | collective-permute-start | bytes 1474568 | tf_op jit(solution)/shard_map/ppermute | solution.py:69
  316.2 85.9 %copy-start.4 = (f32[1280,768]{1,0:T(8,128)}, f32[1280,768]{1,0:T(8,128)S(1)}, u32[]{:S(2)}) copy-start(f32[1280,768]{1,0:T(8,128)S(1)} %get-tuple-element.129) | copy-start | bytes 11796484
  334.4 15.9 %copy-start.50 = (bf16[4,1280,768]{2,1,0:T(8,128)(2,1)}, bf16[4,1280,768]{2,1,0:T(8,128)(2,1)S(1)}, u32[]{:S(2)}) copy-start(bf16[4,1280,768]{2,1,0:T(8,128)(2,1)S(1)} %get-tuple-element.131) | copy-start | bytes 23592964
  351.6 122.2 %collective-permute-start.6 = (bf16[320,768]{1,0:T(8,128)(2,1)}, bf16[320,768]{1,0:T(8,128)(2,1)}, u32[]{:S(2)}, u32[]{:S(2)}) collective-permute-start(bf16[320,768]{1,0:T(8,128)(2,1)} %get-tuple-element.109), channel_id=1, source_target_pairs={{0,0},{4,1},{1,2},{5,3},{2,4},{6,5},{3,6},{7,7},{8,8},{12,9},{9,10... | collective-permute-start | bytes 1474568 | tf_op jit(solution)/shard_map/ppermute | solution.py:84
  353.5 123.6 %collective-permute-start.7 = (bf16[320,768]{1,0:T(8,128)(2,1)}, bf16[320,768]{1,0:T(8,128)(2,1)}, u32[]{:S(2)}, u32[]{:S(2)}) collective-permute-start(bf16[320,768]{1,0:T(8,128)(2,1)} %get-tuple-element.108), channel_id=1, source_target_pairs={{4,0},{0,1},{5,2},{1,3},{6,4},{2,5},{7,6},{3,7},{12,8},{8,9},{13,1... | collective-permute-start | bytes 1474568 | tf_op jit(solution)/shard_map/ppermute | solution.py:84
  356.3 122.7 %collective-permute-start.8 = (bf16[320,768]{1,0:T(8,128)(2,1)}, bf16[320,768]{1,0:T(8,128)(2,1)}, u32[]{:S(2)}, u32[]{:S(2)}) collective-permute-start(bf16[320,768]{1,0:T(8,128)(2,1)} %get-tuple-element.107), channel_id=1, source_target_pairs={{1,0},{5,1},{0,2},{4,3},{3,4},{7,5},{2,6},{6,7},{9,8},{13,9},{8,10... | collective-permute-start | bytes 1474568 | tf_op jit(solution)/shard_map/ppermute | solution.py:84
  356.4 124.5 %collective-permute-start.9 = (bf16[320,768]{1,0:T(8,128)(2,1)}, bf16[320,768]{1,0:T(8,128)(2,1)}, u32[]{:S(2)}, u32[]{:S(2)}) collective-permute-start(bf16[320,768]{1,0:T(8,128)(2,1)} %get-tuple-element.106), channel_id=1, source_target_pairs={{5,0},{1,1},{4,2},{0,3},{7,4},{3,5},{6,6},{2,7},{13,8},{9,9},{12,1... | collective-permute-start | bytes 1474568 | tf_op jit(solution)/shard_map/ppermute | solution.py:84
  362.4 39.7 %copy-start.18 = (bf16[320,768]{1,0:T(8,128)(2,1)}, bf16[320,768]{1,0:T(8,128)(2,1)S(1)}, u32[]{:S(2)}) copy-start(bf16[320,768]{1,0:T(8,128)(2,1)S(1)} %get-tuple-element.113) | copy-start | bytes 1474564
  385.3 16.8 %copy-start.49 = (bf16[4,1280,768]{2,1,0:T(8,128)(2,1)}, bf16[4,1280,768]{2,1,0:T(8,128)(2,1)S(1)}, u32[]{:S(2)}) copy-start(bf16[4,1280,768]{2,1,0:T(8,128)(2,1)S(1)} %multiply_convert_fusion.1) | copy-start | bytes 23592964
  402.1 6.4 copy-start.47
  485.6 45.9 %collective-permute-start.10 = (bf16[4,2,4,80,768]{4,3,2,1,0:T(8,128)(2,1)}, bf16[4,2,4,80,768]{4,3,2,1,0:T(8,128)(2,1)}, u32[]{:S(2)}, u32[]{:S(2)}) collective-permute-start(bf16[4,2,4,80,768]{4,3,2,1,0:T(8,128)(2,1)} %get-tuple-element.63), channel_id=1, source_target_pairs={{0,4},{4,0},{1,5},{5,1},{2,6},{6,2},{3,7},{7,3},{8,12},{12,8},{9,1... | collective-permute-start | bytes 11796488 | tf_op jit(solution)/shard_map/ppermute | solution.py:35
  485.7 10.2 %copy-start.19 = (bf16[320,768]{1,0:T(8,128)(2,1)S(1)}, bf16[320,768]{1,0:T(8,128)(2,1)}, u32[]{:S(2)}) copy-start(bf16[320,768]{1,0:T(8,128)(2,1)} %copy-done.18) | copy-start | bytes 1474564
  495.9 18.9 %copy-start.5 = (f32[1280,768]{1,0:T(8,128)S(1)}, f32[1280,768]{1,0:T(8,128)}, u32[]{:S(2)}) copy-start(f32[1280,768]{1,0:T(8,128)} %copy-done.4) | copy-start | bytes 11796484
  495.9 35.6 %slice-start = ((s8[5898240]{0:T(1024)(128)(4,1)}), s8[4194304]{0:T(1024)(128)(4,1)S(1)}, s32[]{:S(2)}) async-start(s8[5898240]{0:T(1024)(128)(4,1)} %bitcast.148), calls=%async_computation | async-start | bytes 8388608
  514.8 16.7 %slice-start.1 = ((s8[5898240]{0:T(1024)(128)(4,1)}), s8[1703936]{0:T(1024)(128)(4,1)S(1)}, s32[]{:S(2)}) async-start(s8[5898240]{0:T(1024)(128)(4,1)} %bitcast.148), calls=%async_computation.1 | async-start | bytes 3407872
  535.4 15.0 %copy-start.3 = (bf16[4,3,4,80,768]{4,3,2,1,0:T(8,128)(2,1)}, bf16[4,3,4,80,768]{4,3,2,1,0:T(8,128)(2,1)S(1)}, u32[]{:S(2)}) copy-start(bf16[4,3,4,80,768]{4,3,2,1,0:T(8,128)(2,1)S(1)} %pad_maximum_fusion) | copy-start | bytes 17694724
  779.5 5.1 copy-start.6
  779.6 5.1 copy-start.12
  784.6 5.9 copy-start.21
  785.9 5.4 copy-start.9
  787.2 5.2 copy-start.10
  788.1 5.3 copy-start.40
  788.1 5.9 copy-start.39
  (32 other events, 105.7 us)
